TPU v7x, 1024 devices: a whole 8x8x8 slice. The times are simulated.
1024 devices in a mesh: gx: 128 (over z, y, core), gy: 8 (over x).
Axes of the slice: x: 8, y: 8, z: 8, core: 2. Of those that a mesh axis runs over, the one named last changes fastest.
Arguments:
- populations: float32 [27, 256, 64, 128], P(None, 'gx', 'gy'), as said below
- relax: float32 [27], replicated, may hold values from 0.6 to 1.9
- solid: int32 [256, 64, 128], P('gx', 'gy'), may hold values 0 or 1
- wall_cell: int32 [128, 8, 512], P('gx', 'gy'), may hold values from 0 to 2047, as said below
- wall_normal: int32 [128, 8, 512], P('gx', 'gy'), may hold values from 0 to 5
- wall_count: int32 [128, 8], P('gx', 'gy'), may hold values from 1 to 512, as said below
- sample_ref: int32 [128, 8, 512], P('gx', 'gy'), may hold values from 0 to 511, each once within a row
- stencil_cell: int32 [128, 8, 8, 512], P('gx', 'gy'), may hold values from 0 to 2047, as said below
- stencil_weight: float32 [128, 8, 8, 512], P('gx', 'gy'), may hold values from 0 to 1, as said below
Outputs:
- read: float32 [27, 256, 64, 128], P(None, 'gx', 'gy')
Inputs may be any that keep to these rules, and one draw needn't show every extreme that they name: `populations`: positive everywhere. `wall_cell`: the 512 entries of one device are distinct local cells. Slots 0 to wall_count - 1 of a device are live; some device has all 512 live. `stencil_cell`: the eight corners of a unit cube of the owner's local cells, wrapping along z only. `stencil_weight`: nonnegative trilinear weights, summing to one over the eight corners.
All inputs are finite; a program needn't handle non-finite values. No bound on the sum of `solid` on one device may be relied on, other than what follows from the above.
Results may differ from a plain program's by a relative error of at most 0.0003.
Values sent between devices are 32-bit elements; how exact they have to be, the bound alone decides.
A program may use at most 32 MiB of HBM per device.

v0:
```python
import jax
import jax.numpy as jnp
import numpy as np
from jax import lax
from jax.sharding import PartitionSpec as P

lattice_steps = [(a - 1, b - 1, c - 1) for a in range(3) for b in range(3) for c in range(3)]
wall_ratio = (1.0 / 9.0) ** (1.0 / 7.0)


def padded_2(shard, sides, width):
    for axis, dim in sides:
        devices, length = (lax.axis_size(axis), shard.shape[dim])
        up = [(i, (i + 1) % devices) for i in range(devices)]
        down = [(j, i) for i, j in up]
        last = lax.slice_in_dim(shard, length - width, length, axis=dim)
        initial = lax.slice_in_dim(shard, 0, width, axis=dim)
        before = lax.ppermute(last, axis, up)
        after = lax.ppermute(initial, axis, down)
        shard = jnp.concatenate([before, shard, after], axis=dim)
    return shard


def lattice():
    steps = np.array(lattice_steps).T
    single = np.where(steps == 0, 2.0 / 3.0, 1.0 / 6.0)
    weights = np.prod(single, axis=0)
    vander = np.array([[1.0, 1.0, 1.0], [-1.0, 0.0, 1.0], [1.0, 0.0, 1.0]])
    undo = np.array([[0.0, -0.5, 0.5], [1.0, 0.0, -1.0], [0.0, 0.5, 0.5]])
    moment = np.kron(np.kron(vander, vander), vander)
    inverse = np.kron(np.kron(undo, undo), undo)
    return (
        jnp.asarray(steps, jnp.float32),
        jnp.asarray(weights, jnp.float32),
        jnp.asarray(moment, jnp.float32),
        jnp.asarray(inverse, jnp.float32),
    )


def moments(pops):
    steps, weights, moment, inverse = lattice()
    scaled = weights[:, None] * pops
    density = jnp.sum(scaled, axis=0)
    momentum = jnp.dot(steps, scaled, precision=lax.Precision.HIGHEST)
    return (density, momentum / density[None])


def equilibrium(density, velocity):
    steps, weights, moment, inverse = lattice()
    projected = jnp.dot(steps.T, velocity, precision=lax.Precision.HIGHEST)
    speed_sq = jnp.sum(velocity * velocity, axis=0)
    return density[None] * (
        1.0 + 3.0 * projected + 4.5 * projected * projected - 1.5 * speed_sq[None]
    )


def collide(pops, relax):
    steps, weights, moment, inverse = lattice()
    scaled = weights[:, None] * pops
    density, velocity = moments(pops)
    balance = weights[:, None] * equilibrium(density, velocity)
    deviation = jnp.dot(moment, scaled - balance, precision=lax.Precision.HIGHEST) * relax[:, None]
    after = scaled - jnp.dot(inverse, deviation, precision=lax.Precision.HIGHEST)
    return after / weights[:, None]


def sample_velocity(velocity, corner_cells, corner_weight):
    picked = velocity[:, corner_cells]
    return jnp.sum(picked * corner_weight[None], axis=1)


def rebuild_columns(columns, density, velocity, normal, live, picked):
    axis_index = normal // 2
    sign = (2 * (normal % 2) - 1).astype(jnp.float32)
    normal_vec = (jnp.arange(3, dtype=jnp.int32)[:, None] == axis_index[None]).astype(
        jnp.float32
    ) * sign[None]
    along = jnp.sum(picked * normal_vec, axis=0)
    tangential = picked - along[None] * normal_vec
    wall_eq = equilibrium(density, wall_ratio * tangential)
    local_eq = equilibrium(density, velocity)
    return jnp.where(live[None], wall_eq + columns - local_eq, columns)


def stream(padded, post):
    chans, size_x, size_y, size_z = post.shape
    outputs = []
    for direction in range(27):
        step_x, step_y, step_z = lattice_steps[direction]
        moved = padded[
            direction, 1 - step_x : 1 - step_x + size_x, 1 - step_y : 1 - step_y + size_y
        ]
        blocked = padded[27, 1 - step_x : 1 - step_x + size_x, 1 - step_y : 1 - step_y + size_y]
        moved = jnp.roll(moved, step_z, axis=2)
        blocked = jnp.roll(blocked, step_z, axis=2)
        outputs.append(jnp.where(blocked > 0.5, post[26 - direction], moved))
    return jnp.stack(outputs)


def local(
    populations,
    relax,
    solid,
    wall_cell,
    wall_normal,
    wall_count,
    sample_ref,
    stencil_cell,
    stencil_weight,
):
    chans, size_x, size_y, size_z = populations.shape
    flat = populations.reshape(27, size_x * size_y * size_z)
    density, velocity = moments(flat)
    samples = sample_velocity(velocity, stencil_cell[0, 0], stencil_weight[0, 0])
    peers = lax.axis_size("gy")
    received = lax.all_to_all(
        samples.reshape(3, peers, -1), "gy", split_axis=1, concat_axis=1, tiled=True
    ).reshape(3, -1)
    picked = received[:, sample_ref[0, 0]]
    walls = wall_cell[0, 0]
    normal = wall_normal[0, 0]
    live = jnp.arange(walls.shape[0], dtype=jnp.int32) < wall_count[0, 0]
    columns = rebuild_columns(
        flat[:, walls], density[walls], velocity[:, walls], normal, live, picked
    )
    post = collide(flat.at[:, walls].set(columns), relax)
    post_grid = post.reshape(27, size_x, size_y, size_z)
    stacked = jnp.concatenate([post_grid, solid.astype(jnp.float32)[None]], axis=0)
    padded = padded_2(stacked, (("gx", 1), ("gy", 2)), 1)
    return stream(padded, post_grid)


def solution(mesh):
    return jax.shard_map(
        local,
        mesh=mesh,
        in_specs=(
            P(None, "gx", "gy", None),
            P(),
            P("gx", "gy", None),
            P("gx", "gy", None),
            P("gx", "gy", None),
            P("gx", "gy"),
            P("gx", "gy", None),
            P("gx", "gy", None, None),
            P("gx", "gy", None, None),
        ),
        out_specs=P(None, "gx", "gy", None),
        check_vma=False,
    )
```

profile of v0, /device:TPU:6, one launch (start us, length us, event | category | flops | bytes accessed | tf_op | source)
XLA Modules:
  0.0 82.0 jit_solution(3854603007841572390)
XLA Ops:
  0.0 1.0 %pad.253 = f32[32,16,128]{2,1,0:T(8,128)S(1)} pad(f32[27,16,128]{2,1,0:T(8,128)} %bitcast.287, f32[]{:T(128)} %constant.24.clone.1), padding=0_5x0_0x0_0 | pad | bytes 483332
  1.1 1.0 %multiply_reduce_fusion.3 = f32[2,8,128]{2,1,0:T(8,128)S(1)} fusion(f32[27,2,8,128]{3,2,1,0:T(8,128)} %param.19, f32[27]{0:T(128)} %constant.64.clone), kind=kLoop, calls=%fused_computation.33 | loop fusion | flops 108544 | bytes 229484 | tf_op jit(solution)/shard_map/reduce_sum | solution.py:43
  2.1 1.0 %fusion.1 = f32[3,2048]{1,0:T(4,128)S(1)} fusion(f32[3,27]{1,0:T(4,128)} %constant.63.clone, f32[27,2048]{1,0:T(8,128)S(1)} %bitcast.280, f32[27]{0:T(128)} %constant.64.clone, f32[2048]{0:T(1024)S(1)} %bitcast.278), kind=kOutput, calls=%fused_computation.11 | convolution fusion | flops 2052096 | bytes 254384 | tf_op jit(solution)/shard_map/dot_general | solution.py:44
  3.6 10.8 %gather_fusion.1 = f32[4096,3]{1,0:T(8,128)S(1)} fusion(f32[3,2048]{0,1:T(8,128)S(1)} %copy.195, s32[4096]{0:T(1024)S(1)} %broadcast_clamp_fusion), kind=kCustom, calls=%fused_computation.1 | custom fusion | bytes 114688 | tf_op jit(solution)/shard_map/gather | solution.py:68
  14.4 1.4 %multiply_reduce_fusion = f32[512,3]{1,0:T(8,128)} fusion(f32[8,512,3]{2,1,0:T(8,128)S(1)} %bitcast.282, f32[8,512]{1,0:T(8,128)S(1)} %bitcast.325), kind=kLoop, calls=%fused_computation.12 | loop fusion | flops 23040 | bytes 71680 | tf_op jit(solution)/shard_map/reduce_sum | solution.py:69
  15.8 1.1 %copy.197 = f32[3,8,64]{2,0,1:T(4,128)S(1)} copy(f32[3,8,64]{0,2,1:T(8,128)} %bitcast.284) | data formatting | bytes 12288 | tf_op jit(solution)/shard_map/reshape | solution.py:117
  16.9 0.7 reshape.1466
  17.6 16.4 %all-to-all-start = ((f32[8,1,192]{2,1,0:T(1,128)}), f32[8,1,192]{2,1,0:T(1,128)S(1)}, u32[]{:S(2)}, u32[]{:S(2)}) async-start(f32[8,1,192]{2,1,0:T(1,128)} %reshape.1466), calls=%async_computation | async-start | bytes 16384 | tf_op jit(solution)/shard_map/all_to_all | solution.py:116
  34.2 1.0 %gather_fusion.4 = f32[512,3]{1,0:T(8,128)S(1)} fusion(f32[3,2048]{0,1:T(8,128)S(1)} %copy.195, s32[1024]{0:T(1024)S(1)} %get-tuple-element.108), kind=kCustom, calls=%fused_computation.4 | custom fusion | bytes 14336 | tf_op jit(solution)/shard_map/gather | solution.py:124
  36.4 3.1 %gather_fusion = f32[512]{0:T(512)S(1)} fusion(f32[2048]{0:T(1024)S(1)} %bitcast.279, s32[1024]{0:T(1024)S(1)} %get-tuple-element.108), kind=kCustom, calls=%fused_computation | custom fusion | bytes 6144 | tf_op jit(solution)/shard_map/gather | solution.py:124
  39.6 1.0 %gather_fusion.3 = f32[512,27]{1,0:T(8,128)S(1)} fusion(f32[27,2048]{0,1:T(8,128)S(1)} %copy.202, s32[1024]{0:T(1024)S(1)} %get-tuple-element.108), kind=kCustom, calls=%fused_computation.3 | custom fusion | bytes 112640 | tf_op jit(solution)/shard_map/gather | solution.py:124
  40.7 0.5 broadcast.383
  41.3 0.7 reduce.5
  42.2 1.0 %gather_fusion.2 = f32[512,3]{1,0:T(8,128)S(1)} fusion(f32[3,512]{0,1:T(8,128)S(1)} %bitcast.288, s32[1024]{0:T(1024)S(1)} %get-tuple-element.107), kind=kCustom, calls=%fused_computation.2 | custom fusion | bytes 14336 | tf_op jit(solution)/shard_map/gather | solution.py:119
  43.9 0.6 fusion.16
  45.1 2.1 %scatter_fusion = f32[27,2048]{0,1:T(8,128)S(1)} fusion(f32[27,2048]{0,1:T(8,128)S(1)} %copy.202, s32[512]{0:T(512)S(1)} %bitcast.324, f32[512,27]{1,0:T(8,128)S(1)} %copy.203), kind=kCustom, calls=%fused_computation.5 | custom fusion | bytes 167936 | tf_op jit(solution)/shard_map/scatter | solution.py:126
  49.8 1.9 %collective-permute-start = (f32[28,1,8,128]{3,2,1,0:T(8,128)S(1)}, f32[28,1,8,128]{3,2,1,0:T(8,128)S(1)}, u32[]{:S(2)}, u32[]{:S(2)}) collective-permute-start(f32[28,1,8,128]{3,2,1,0:T(8,128)S(1)} %get-tuple-element.63), channel_id=1, source_target_pairs={{0,8},{8,16},{16,24},{24,32},{32,40},{40,48},{48,56},{56,64},{64,7... | collective-permute-start | bytes 344072 | tf_op jit(solution)/shard_map/ppermute | solution.py:18
  51.7 10.8 %collective-permute-start.1 = (f32[28,1,8,128]{3,2,1,0:T(8,128)S(1)}, f32[28,1,8,128]{3,2,1,0:T(8,128)S(1)}, u32[]{:S(2)}, u32[]{:S(2)}) collective-permute-start(f32[28,1,8,128]{3,2,1,0:T(8,128)S(1)} %get-tuple-element.64), channel_id=1, source_target_pairs={{8,0},{16,8},{24,16},{32,24},{40,32},{48,40},{56,48},{64,56},{72,6... | collective-permute-start | bytes 344072 | tf_op jit(solution)/shard_map/ppermute | solution.py:19
  63.0 1.8 %collective-permute-done.1 = f32[28,1,8,128]{3,2,1,0:T(8,128)S(1)} collective-permute-done((f32[28,1,8,128]{3,2,1,0:T(8,128)S(1)}, f32[28,1,8,128]{3,2,1,0:T(8,128)S(1)}, u32[]{:S(2)}, u32[]{:S(2)}) %collective-permute-start.1) | collective-permute-done | bytes 114720 | tf_op jit(solution)/shard_map/ppermute | solution.py:19
  64.9 4.6 %collective-permute-start.3 = (f32[28,4,1,128]{3,2,1,0:T(1,128)S(1)}, f32[28,4,1,128]{3,2,1,0:T(1,128)S(1)}, u32[]{:S(2)}, u32[]{:S(2)}) collective-permute-start(f32[28,4,1,128]{3,2,1,0:T(1,128)S(1)} %get-tuple-element.27), channel_id=1, source_target_pairs={{0,1},{1,2},{2,3},{3,4},{4,5},{5,6},{6,7},{7,0},{8,9},{9,10},{10,1... | collective-permute-start | bytes 172040 | tf_op jit(solution)/shard_map/ppermute | solution.py:18
  69.6 1.9 %collective-permute-start.2 = (f32[28,4,1,128]{3,2,1,0:T(1,128)S(1)}, f32[28,4,1,128]{3,2,1,0:T(1,128)S(1)}, u32[]{:S(2)}, u32[]{:S(2)}) collective-permute-start(f32[28,4,1,128]{3,2,1,0:T(1,128)S(1)} %get-tuple-element.28), channel_id=1, source_target_pairs={{1,0},{2,1},{3,2},{4,3},{5,4},{6,5},{7,6},{0,7},{9,8},{10,9},{11,1... | collective-permute-start | bytes 172040 | tf_op jit(solution)/shard_map/ppermute | solution.py:19
  71.6 5.2 %collective-permute-done.2 = f32[28,4,1,128]{3,2,1,0:T(1,128)S(1)} collective-permute-done((f32[28,4,1,128]{3,2,1,0:T(1,128)S(1)}, f32[28,4,1,128]{3,2,1,0:T(1,128)S(1)}, u32[]{:S(2)}, u32[]{:S(2)}) %collective-permute-start.2) | collective-permute-done | bytes 57376 | tf_op jit(solution)/shard_map/ppermute | solution.py:19
  80.7 0.6 copy-done.10
  81.3 0.7 constant_dynamic-update-slice_fusion
  (148 shorter events, 9.6 us)
Async XLA Ops:
  0.0 3.6 %copy-start.3 = (s32[1,1,8,512]{3,2,1,0:T(8,128)S(1)}, s32[1,1,8,512]{3,2,1,0:T(8,128)}, u32[]{:S(2)}) copy-start(s32[1,1,8,512]{3,2,1,0:T(8,128)} %param.26) | copy-start | bytes 49156
  0.0 14.4 %copy-start.1 = (f32[1,1,8,512]{3,2,1,0:T(8,128)S(1)}, f32[1,1,8,512]{3,2,1,0:T(8,128)}, u32[]{:S(2)}) copy-start(f32[1,1,8,512]{3,2,1,0:T(8,128)} %param.27) | copy-start | bytes 49156
  3.2 30.8 %copy-start.5 = (s32[2,8,128]{2,1,0:T(8,128)S(1)}, s32[2,8,128]{2,1,0:T(8,128)}, u32[]{:S(2)}) copy-start(s32[2,8,128]{2,1,0:T(8,128)} %param.21) | copy-start | bytes 24580
  3.2 30.9 %copy-start.7 = (s32[1,1,512]{2,1,0:T(1,128)S(1)}, s32[1,1,512]{2,1,0:T(1,128)}, u32[]{:S(2)}) copy-start(s32[1,1,512]{2,1,0:T(1,128)} %param.22) | copy-start | bytes 6148
  3.2 30.9 %copy-start.8 = (s32[1,1,512]{2,1,0:T(1,128)S(1)}, s32[1,1,512]{2,1,0:T(1,128)}, u32[]{:S(2)}) copy-start(s32[1,1,512]{2,1,0:T(1,128)} %param.25) | copy-start | bytes 6148
  3.2 30.9 %copy-start.6 = (s32[1,1,512]{2,1,0:T(1,128)S(1)}, s32[1,1,512]{2,1,0:T(1,128)}, u32[]{:S(2)}) copy-start(s32[1,1,512]{2,1,0:T(1,128)} %param.23) | copy-start | bytes 6148
  17.6 23.1 %all-to-all-start = ((f32[8,1,192]{2,1,0:T(1,128)}), f32[8,1,192]{2,1,0:T(1,128)S(1)}, u32[]{:S(2)}, u32[]{:S(2)}) async-start(f32[8,1,192]{2,1,0:T(1,128)} %reshape.1466), calls=%async_computation | async-start | bytes 16384 | tf_op jit(solution)/shard_map/all_to_all | solution.py:116
  36.4 7.5 %copy-start = (f32[3,27]{1,0:T(4,128)S(1)}, f32[3,27]{1,0:T(4,128)}, u32[]{:S(2)}) copy-start(f32[3,27]{1,0:T(4,128)} %constant.63.clone) | copy-start | bytes 976
  43.2 4.4 %copy-start.4 = (f32[27]{0:T(128)S(1)}, f32[27]{0:T(128)}, u32[]{:S(2)}) copy-start(f32[27]{0:T(128)} %constant.64.clone) | copy-start | bytes 328
  44.5 4.0 %copy-start.11 = (f32[27]{0:T(128)S(1)}, f32[27]{0:T(128)}, u32[]{:S(2)}) copy-start(f32[27]{0:T(128)} %param.20) | copy-start | bytes 328
  44.5 4.0 %copy-start.12 = (f32[27,27]{1,0:T(8,128)S(1)}, f32[27,27]{1,0:T(8,128)}, u32[]{:S(2)}) copy-start(f32[27,27]{1,0:T(8,128)} %constant.65.clone) | copy-start | bytes 8752
  45.1 3.9 %copy-start.2 = (f32[27,27]{1,0:T(8,128)S(1)}, f32[27,27]{1,0:T(8,128)}, u32[]{:S(2)}) copy-start(f32[27,27]{1,0:T(8,128)} %constant.66.clone) | copy-start | bytes 8752
  45.1 3.9 %copy-start.9 = (f32[27]{0:T(128)S(1)}, f32[27]{0:T(128)}, u32[]{:S(2)}) copy-start(f32[27]{0:T(128)} %constant.75) | copy-start | bytes 328
  49.8 13.2 %collective-permute-start = (f32[28,1,8,128]{3,2,1,0:T(8,128)S(1)}, f32[28,1,8,128]{3,2,1,0:T(8,128)S(1)}, u32[]{:S(2)}, u32[]{:S(2)}) collective-permute-start(f32[28,1,8,128]{3,2,1,0:T(8,128)S(1)} %get-tuple-element.63), channel_id=1, source_target_pairs={{0,8},{8,16},{16,24},{24,32},{32,40},{40,48},{48,56},{56,64},{64,7... | collective-permute-start | bytes 344072 | tf_op jit(solution)/shard_map/ppermute | solution.py:18
  51.7 13.1 %collective-permute-start.1 = (f32[28,1,8,128]{3,2,1,0:T(8,128)S(1)}, f32[28,1,8,128]{3,2,1,0:T(8,128)S(1)}, u32[]{:S(2)}, u32[]{:S(2)}) collective-permute-start(f32[28,1,8,128]{3,2,1,0:T(8,128)S(1)} %get-tuple-element.64), channel_id=1, source_target_pairs={{8,0},{16,8},{24,16},{32,24},{40,32},{48,40},{56,48},{64,56},{72,6... | collective-permute-start | bytes 344072 | tf_op jit(solution)/shard_map/ppermute | solution.py:19
  64.9 6.6 %collective-permute-start.3 = (f32[28,4,1,128]{3,2,1,0:T(1,128)S(1)}, f32[28,4,1,128]{3,2,1,0:T(1,128)S(1)}, u32[]{:S(2)}, u32[]{:S(2)}) collective-permute-start(f32[28,4,1,128]{3,2,1,0:T(1,128)S(1)} %get-tuple-element.27), channel_id=1, source_target_pairs={{0,1},{1,2},{2,3},{3,4},{4,5},{5,6},{6,7},{7,0},{8,9},{9,10},{10,1... | collective-permute-start | bytes 172040 | tf_op jit(solution)/shard_map/ppermute | solution.py:18
  69.6 7.3 %collective-permute-start.2 = (f32[28,4,1,128]{3,2,1,0:T(1,128)S(1)}, f32[28,4,1,128]{3,2,1,0:T(1,128)S(1)}, u32[]{:S(2)}, u32[]{:S(2)}) collective-permute-start(f32[28,4,1,128]{3,2,1,0:T(1,128)S(1)} %get-tuple-element.28), channel_id=1, source_target_pairs={{1,0},{2,1},{3,2},{4,3},{5,4},{6,5},{7,6},{0,7},{9,8},{10,9},{11,1... | collective-permute-start | bytes 172040 | tf_op jit(solution)/shard_map/ppermute | solution.py:19
  80.6 0.7 copy-start.10
where the time goes:
time: 82.3 us; the launch traced here: 82 us
  starting transfers between devices  35.5 us (43%)
  local copies, waits for them, and re-layouts  27.6 us (34%)
  waiting for transfers between devices  7.58 us (9%)
  other arithmetic  6.32 us (8%)
  matrix products  3.66 us (4%)
  between operations  1.29 us (2%)
    all_to_all x1, starting transfers between devices, local(): lax.all_to_all(samples.reshape(3, peers, -1), 'gy', split_axis=1, concat_...  16.4 us
    ppermute x2, starting transfers between devices, padded_2(): after = lax.ppermute(initial, axis, down)  12.7 us
    gather x1, local copies, waits for them, and re-layouts, sample_velocity(): picked = velocity[:, corner_cells]  10.8 us
    ppermute x2, waiting for transfers between devices, padded_2(): after = lax.ppermute(initial, axis, down)  7.05 us
    ppermute x2, starting transfers between devices, padded_2(): before = lax.ppermute(last, axis, up)  6.5 us
    gather x1, local copies, waits for them, and re-layouts, local(): density[walls]  3.14 us
    unnamed x33, local copies, waits for them, and re-layouts  2.56 us
    scatter x2, local copies, waits for them, and re-layouts, local(): post = collide(flat.at[:, walls].set(columns), relax)  2.45 us
  transfers between devices with their start and end apart: 5, of which 3 were waited for; matrix products, arithmetic and copies ran while one was open for 8% of the time, Pallas kernels for 0%

commit v1 on v0

v1 whole, which is shorter than its diff:
```python
import jax
import jax.numpy as jnp
import numpy as np
from jax import lax
from jax.experimental import pallas as pl
from jax.experimental.pallas import tpu as pltpu
from jax.sharding import PartitionSpec as P

MESH = pl.DeviceIdType.MESH
wall_ratio = (1.0 / 9.0) ** (1.0 / 7.0)
steps = [(a, b, c) for a in (-1, 0, 1) for b in (-1, 0, 1) for c in (-1, 0, 1)]
index_of = {e: i for i, e in enumerate(steps)}
weight = [float(np.prod([2.0 / 3.0 if v == 0 else 1.0 / 6.0 for v in e])) for e in steps]
F32 = jnp.float32
I32 = jnp.int32


def along(values, axis, combine):
    stride = (9, 3, 1)[axis]
    out = list(values)
    for i in range(27):
        if i // stride % 3 == 0:
            out[i], out[i + stride], out[i + 2 * stride] = combine(
                values[i], values[i + stride], values[i + 2 * stride]
            )
    return out


def to_moments(lo, mid, hi):
    both = hi + lo
    return both + mid, hi - lo, both


def from_moments(zero, one, two):
    return two - one, zero - two, two + one


def equilibrium_moments(rho, vel):
    sq = [v * v for v in vel]
    third = 1.0 / 3.0
    out = []
    for powers in [(a, b, c) for a in range(3) for b in range(3) for c in range(3)]:
        odd = [k for k in range(3) if powers[k] == 1]
        even = [k for k in range(3) if powers[k] == 2]
        scale = third ** len(even)
        if len(odd) == 3:
            out.append(None)
        elif len(odd) == 2:
            out.append(rho * (vel[odd[0]] * vel[odd[1]] * scale))
        elif len(odd) == 1:
            out.append(rho * (vel[odd[0]] * scale))
        elif not even:
            out.append(rho)
        else:
            total = sq[even[0]]
            for k in even[1:]:
                total = total + sq[k]
            out.append(rho * (scale + 3.0 * scale * total))
    return out


def shifted(value, b, c):
    if c:
        value = pltpu.roll(value, c % 128, 1)
    if b:
        value = pltpu.roll(value, b % 8, 0)
    return value


def lane_gather(table, index):
    return jnp.take_along_axis(table, index, axis=1, mode="promise_in_bounds")


def row_of(ref, lead, row):
    return jnp.broadcast_to(ref[lead + (slice(row, row + 1), slice(None))], (8, 128))


def body(
    n_gx,
    n_gy,
    pop_h,
    relax_s,
    solid_h,
    cell_h,
    normal_h,
    count_s,
    ref_h,
    corner_h,
    cweight_h,
    out,
    pop,
    solid,
    cell,
    normal,
    sref,
    corner,
    cweight,
    part,
    fields,
    code,
    blocked,
    sample,
    sample_in,
    solid_x,
    solid_y,
    solid_d,
    face,
    face_in,
    rows,
    rows_in,
    rows_d,
    rolled,
    posts,
    in_sem,
    s_send,
    s_recv,
    o_send,
    o_recv,
    h_send,
    h_recv,
):
    p = lax.axis_index("gx")
    q = lax.axis_index("gy")
    px = [lax.rem(p + n_gx + a, n_gx) for a in (-1, 0, 1)]
    qy = [lax.rem(q + n_gy + b, n_gy) for b in (-1, 0, 1)]

    loads = [
        pltpu.make_async_copy(src, dst, in_sem.at[k])
        for k, (src, dst) in enumerate(
            [
                (pop_h, pop),
                (corner_h, corner),
                (cweight_h, cweight),
                (solid_h, solid),
                (cell_h, cell),
                (normal_h, normal),
                (ref_h, sref),
            ]
        )
    ]
    for copy in loads:
        copy.start()

    barrier = pltpu.get_barrier_semaphore()
    ring = [(p, lax.rem(q + k, n_gy)) for k in range(1, n_gy)]
    side = [(px[a + 1], qy[b + 1]) for a in (-1, 1) for b in (-1, 0, 1)]
    for peer in ring + side:
        pl.semaphore_signal(barrier, inc=1, device_id=peer, device_id_type=MESH)

    row_id = lax.broadcasted_iota(I32, (8, 128), 0)

    loads[0].wait()
    vel = []
    for x in range(2):
        f = [pop[i, x] * weight[i] for i in range(27)]
        for axis in (2, 1, 0):
            f = along(f, axis, to_moments)
        rho = f[0]
        inv = 1.0 / rho
        u = [f[9] * inv, f[3] * inv, f[1] * inv]
        vel.append(u)
        fields[0, x] = rho
        for k in range(3):
            fields[k + 1, x] = u[k]
        balance = equilibrium_moments(rho, u)
        for m in range(27):
            off = f[m] if balance[m] is None else f[m] - balance[m]
            f[m] = off * (1.0 - relax_s[m])
        for axis in (2, 1, 0):
            f = along(f, axis, from_moments)
        for i, e in enumerate(steps):
            part[i, x] = f[i] * float(np.prod([1.5 if v == 0 else 3.0 for v in e]))

    loads[1].wait()
    loads[2].wait()
    for j in range(4):
        total = [jnp.zeros((8, 128), F32) for _ in range(3)]
        lanes = slice(128 * j, 128 * (j + 1))
        for k in range(8):
            where = jnp.broadcast_to(corner[0, 0, k : k + 1, lanes], (8, 128))
            share = jnp.broadcast_to(cweight[0, 0, k : k + 1, lanes], (8, 128))
            lane = where & 127
            mine = jnp.where((where >> 7) & 7 == row_id, share, 0.0)
            upper = where >= 1024
            for n in range(3):
                got = jnp.where(upper, lane_gather(vel[1][n], lane), lane_gather(vel[0][n], lane))
                total[n] = total[n] + mine * got
        for n in range(3):
            sample[j, n : n + 1] = jnp.sum(total[n], axis=0, keepdims=True)

    pl.semaphore_wait(barrier, len(ring) + len(side))

    def send(src, dst, send_sem, recv_sem, peer):
        copy = pltpu.make_async_remote_copy(
            src_ref=src, dst_ref=dst, send_sem=send_sem, recv_sem=recv_sem,
            device_id=peer, device_id_type=MESH,
        )
        copy.start()
        return copy

    sample_copies = [
        send(sample.at[peer[1] // 2], sample_in.at[q], s_send.at[k], s_recv.at[q], peer)
        for k, peer in enumerate(ring)
    ]
    loads[3].wait()
    solid_copies = []
    for n, a in enumerate((1, -1)):
        mine = 1 if a == 1 else 0
        solid_copies.append(
            send(solid.at[mine], solid_x.at[n], o_send.at[n], o_recv.at[n], (px[a + 1], q))
        )
        solid_copies.append(
            send(solid, solid_y.at[n], o_send.at[2 + n], o_recv.at[2 + n], (p, qy[a + 1]))
        )
        for m, b in enumerate((1, -1)):
            k = 4 + 2 * n + m
            solid_copies.append(
                send(solid.at[mine], solid_d.at[n, m], o_send.at[k], o_recv.at[k], (px[a + 1], qy[b + 1]))
            )

    for k in range(4, 7):
        loads[k].wait()
    cells = cell[0]
    live = lax.broadcasted_iota(I32, (1, 512), 1) < count_s[0, 0]
    refs = sref[0]
    first = jnp.where(live, (refs & 63) + 1, 0)
    second = jnp.where(live, (refs >> 6) * 8 + normal[0], 0)
    rows16 = lax.broadcasted_iota(I32, (16, 512), 0) == (cells >> 7)
    left = jnp.concatenate(
        [jnp.where(rows16, first, 0), jnp.where(rows16, second, 0)], axis=0
    ).astype(F32).astype(jnp.bfloat16)
    right = jnp.where(
        lax.broadcasted_iota(I32, (128, 512), 0) == (cells & 127), 1.0, 0.0
    ).astype(jnp.bfloat16)
    code[...] = lax.dot_general(
        left, right, (((1,), (1,)), ((), ())), preferred_element_type=F32
    ).astype(I32)

    for copy in solid_copies:
        copy.wait_recv()
    flags = [solid_x[0], solid[0], solid[1], solid_x[1]]
    for xx in range(4):
        for b in (-1, 0, 1):
            plane = flags[xx]
            if b:
                m = 0 if b == 1 else 1
                near = 7 if b == 1 else 0
                if xx in (1, 2):
                    edge = row_of(solid_y, (m, xx - 1), near)
                else:
                    edge = row_of(solid_d, (0 if xx == 0 else 1, m), near)
                plane = pltpu.roll(plane, b % 8, 0)
                plane = jnp.where(row_id == (0 if b == 1 else 7), edge, plane)
            for c in (-1, 0, 1):
                blocked[xx, 3 * (b + 1) + c + 1] = shifted(plane, 0, c)

    for copy in sample_copies:
        copy.wait_send()
    for k in range(1, n_gy):
        peer = lax.rem(q + n_gy - k, n_gy)
        pltpu.make_async_remote_copy(
            src_ref=sample.at[0], dst_ref=sample_in.at[peer], send_sem=s_send.at[0],
            recv_sem=s_recv.at[peer], device_id=(p, peer), device_id_type=MESH,
        ).wait_recv()
    sample_in[q] = sample[q // 2]

    lane_base = lax.rem(q, 2) * 64 - 1
    for x in range(2):
        first = code[8 * x : 8 * x + 8]
        second = code[16 + 8 * x : 24 + 8 * x]
        lane = jnp.maximum(first + lane_base, 0)
        owner = second >> 3
        axis = (second & 7) >> 1
        picked = [jnp.zeros((8, 128), F32) for _ in range(3)]
        for k in range(n_gy):
            here = owner == k
            for n in range(3):
                got = lane_gather(row_of(sample_in, (k,), n), lane)
                picked[n] = jnp.where(here, got, picked[n])
        rho = fields[0, x]
        u = [
            jnp.where(
                first > 0,
                jnp.where(axis == n, 0.0, wall_ratio * picked[n]),
                fields[n + 1, x],
            )
            for n in range(3)
        ]
        base = rho - 1.5 * rho * (u[0] * u[0] + u[1] * u[1] + u[2] * u[2])
        for i in range(13, 27):
            e = steps[i]
            along_e = None
            for n in range(3):
                if e[n]:
                    term = u[n] if e[n] > 0 else -u[n]
                    along_e = term if along_e is None else along_e + term
            if along_e is None:
                posts[i, x] = part[i, x] + base
                continue
            linear = 3.0 * rho * along_e
            even = base + 1.5 * along_e * linear
            posts[i, x] = part[i, x] + (even + linear)
            posts[26 - i, x] = part[26 - i, x] + (even - linear)

    for i, (a, b, c) in enumerate(steps):
        for x in range(2):
            value = shifted(posts[i, x], b, c)
            inside = 0 <= x + a <= 1
            if inside:
                rolled[i, x] = value
            else:
                face[0 if a == 1 else 1, 3 * (b + 1) + c + 1] = value
            if b:
                m = 0 if b == 1 else 1
                near = 0 if b == 1 else 7
                if inside:
                    r = 4 * (c + 1) + (x if a == 0 else 2 if a == 1 else 3)
                else:
                    r = (16 if a == 1 else 24) + c + 1
                rows[m, r : r + 1] = value[near : near + 1]

    halo_copies = []
    for n, a in enumerate((1, -1)):
        for m, b in enumerate((1, -1)):
            k = 4 + 2 * n + m
            halo_copies.append(
                send(rows.at[m, pl.ds(16 + 8 * n, 8)], rows_d.at[n, m], h_send.at[k], h_recv.at[k],
                     (px[a + 1], qy[b + 1]))
            )
        halo_copies.append(
            send(face.at[n], face_in.at[n], h_send.at[n], h_recv.at[n], (px[a + 1], q))
        )
        halo_copies.append(
            send(rows.at[n, pl.ds(0, 16)], rows_in.at[n], h_send.at[2 + n], h_recv.at[2 + n],
                 (p, qy[a + 1]))
        )
    for copy in halo_copies:
        copy.wait_recv()

    for i, (a, b, c) in enumerate(steps):
        for x in range(2):
            from_x = x - a
            inside = 0 <= from_x <= 1
            n = 0 if a == 1 else 1
            value = rolled[i, from_x] if inside else face_in[n, 3 * (b + 1) + c + 1]
            if b:
                m = 0 if b == 1 else 1
                if inside:
                    r = 4 * (c + 1) + (from_x if a == 0 else 2 if a == 1 else 3)
                    edge = row_of(rows_in, (m,), r)
                else:
                    edge = row_of(rows_d, (n, m), c + 1)
                value = jnp.where(row_id == (0 if b == 1 else 7), edge, value)
            wall = blocked[from_x + 1, 3 * (b + 1) + c + 1]
            out[i, x] = jnp.where(wall != 0, posts[26 - i, x], value)

    for copy in solid_copies + halo_copies:
        copy.wait_send()


def local(*args):
    n_gx, n_gy = lax.axis_size("gx"), lax.axis_size("gy")
    hbm = pl.BlockSpec(memory_space=pl.ANY)
    smem = pl.BlockSpec(memory_space=pltpu.SMEM)
    vmem = pltpu.VMEM
    dma = pltpu.SemaphoreType.DMA
    return pl.pallas_call(
        lambda *refs: body(n_gx, n_gy, *refs),
        name="lattice_step",
        out_shape=jax.ShapeDtypeStruct((27, 2, 8, 128), F32),
        in_specs=[hbm, smem, hbm, hbm, hbm, smem, hbm, hbm, hbm],
        out_specs=pl.BlockSpec(memory_space=pltpu.VMEM),
        scratch_shapes=[
            vmem((27, 2, 8, 128), F32),
            vmem((2, 8, 128), I32),
            vmem((1, 1, 512), I32),
            vmem((1, 1, 512), I32),
            vmem((1, 1, 512), I32),
            vmem((1, 1, 8, 512), I32),
            vmem((1, 1, 8, 512), F32),
            vmem((27, 2, 8, 128), F32),
            vmem((4, 2, 8, 128), F32),
            vmem((32, 128), I32),
            vmem((4, 9, 8, 128), I32),
            vmem((4, 8, 128), F32),
            vmem((n_gy, 8, 128), F32),
            vmem((2, 8, 128), I32),
            vmem((2, 2, 8, 128), I32),
            vmem((2, 2, 8, 128), I32),
            vmem((2, 9, 8, 128), F32),
            vmem((2, 9, 8, 128), F32),
            vmem((2, 32, 128), F32),
            vmem((2, 16, 128), F32),
            vmem((2, 2, 8, 128), F32),
            vmem((27, 2, 8, 128), F32),
            vmem((27, 2, 8, 128), F32),
            dma((7,)),
            dma((n_gy - 1,)),
            dma((n_gy,)),
            dma((8,)),
            dma((8,)),
            dma((8,)),
            dma((8,)),
        ],
        compiler_params=pltpu.CompilerParams(collective_id=0, has_side_effects=True),
    )(*args)


def solution(mesh):
    return jax.shard_map(
        local,
        mesh=mesh,
        in_specs=(
            P(None, "gx", "gy", None),
            P(),
            P("gx", "gy", None),
            P("gx", "gy", None),
            P("gx", "gy", None),
            P("gx", "gy"),
            P("gx", "gy", None),
            P("gx", "gy", None, None),
            P("gx", "gy", None, None),
        ),
        out_specs=P(None, "gx", "gy", None),
        check_vma=False,
    )
```

time: 82.3 us -> 36.5 us (0.44)
  the two profiles are of different devices: /device:TPU:6 before, /device:TPU:1 now
where the time goes in v1:
time: 36.5 us; the launch traced here: 36.3 us
  Pallas kernels  34 us (93%)
  local copies, waits for them, and re-layouts  1.64 us (4%)
  between operations  0.66 us (2%)
    pallas_call x1, Pallas kernels, local(): pl.pallas_call(lambda *refs: body(n_gx, n_gy, *refs), name='lattice_step'...  34 us
    unnamed x1, local copies, waits for them, and re-layouts  1.64 us

profile of v1, /device:TPU:1, one launch (start us, length us, event | category | flops | bytes accessed | tf_op | source)
XLA Modules:
  0.0 36.3 jit_solution(14367269665926225096)
XLA Ops:
  0.7 34.0 %lattice_step.1 = f32[27,2,8,128]{3,2,1,0:T(8,128)} custom-call(f32[27,2,8,128]{3,2,1,0:T(8,128)} %refs_0_.1, f32[27]{0:T(128)} %refs_1_.1, s32[2,8,128]{2,1,0:T(8,128)} %refs_2_.1, s32[1,1,512]{2,1,0:T(1,128)} %refs_3_.1, s32[1,1,512]{2,1,0:T(1,128)} %refs_4_.1, s32[1,1]{1,0:T(1,128)S(6)} %copy.11.refs_5_, s32[1,1,512]{2,1,0:T(1,128)} %refs_6_.1, ...), custom_call_target="tpu_custom_call" | custom-call | tf_op jit(solution)/shard_map/lattice_step/pallas_call | solution.py:367
  34.6 1.6 %copy.12 = f32[27,2,8,128]{3,2,1,0:T(8,128)} copy(f32[27,2,8,128]{3,2,1,0:T(8,128)} %lattice_step.1) | data formatting | bytes 442368

commit v2 on v1

v2 whole, which is shorter than its diff:
```python
import jax
import jax.numpy as jnp
import numpy as np
from jax import lax
from jax.experimental import pallas as pl
from jax.experimental.pallas import tpu as pltpu
from jax.sharding import PartitionSpec as P

MESH = pl.DeviceIdType.MESH
wall_ratio = (1.0 / 9.0) ** (1.0 / 7.0)
steps = [(a, b, c) for a in (-1, 0, 1) for b in (-1, 0, 1) for c in (-1, 0, 1)]
index_of = {e: i for i, e in enumerate(steps)}
weight = [float(np.prod([2.0 / 3.0 if v == 0 else 1.0 / 6.0 for v in e])) for e in steps]
F32 = jnp.float32
I32 = jnp.int32


def along(values, axis, combine):
    stride = (9, 3, 1)[axis]
    out = list(values)
    for i in range(27):
        if i // stride % 3 == 0:
            out[i], out[i + stride], out[i + 2 * stride] = combine(
                values[i], values[i + stride], values[i + 2 * stride]
            )
    return out


def to_moments(lo, mid, hi):
    both = hi + lo
    return both + mid, hi - lo, both


def from_moments(zero, one, two):
    return two - one, zero - two, two + one


def equilibrium_moments(rho, vel):
    sq = [v * v for v in vel]
    third = 1.0 / 3.0
    out = []
    for powers in [(a, b, c) for a in range(3) for b in range(3) for c in range(3)]:
        odd = [k for k in range(3) if powers[k] == 1]
        even = [k for k in range(3) if powers[k] == 2]
        scale = third ** len(even)
        if len(odd) == 3:
            out.append(None)
        elif len(odd) == 2:
            out.append(rho * (vel[odd[0]] * vel[odd[1]] * scale))
        elif len(odd) == 1:
            out.append(rho * (vel[odd[0]] * scale))
        elif not even:
            out.append(rho)
        else:
            total = sq[even[0]]
            for k in even[1:]:
                total = total + sq[k]
            out.append(rho * (scale + 3.0 * scale * total))
    return out


def shifted(value, b, c):
    if c:
        value = pltpu.roll(value, c % 128, 1)
    if b:
        value = pltpu.roll(value, b % 8, 0)
    return value


def lane_gather(table, index):
    return jnp.take_along_axis(table, index, axis=1, mode="promise_in_bounds")


def row_of(ref, lead, row):
    return jnp.broadcast_to(ref[lead + (slice(row, row + 1), slice(None))], (8, 128))


def line(ref, row):
    return jnp.broadcast_to(ref[row], (8, 128))


def total_of(u, e):
    total = None
    for n in range(3):
        if e[n]:
            term = u[n] if e[n] > 0 else -u[n]
            total = term if total is None else total + term
    return total


def body(
    n_gx,
    n_gy,
    pop_h,
    relax_h,
    solid_h,
    cell_h,
    normal_h,
    count_s,
    ref_h,
    corner_h,
    cweight_h,
    out,
    relax_s,
    pop,
    solid,
    cell,
    normal,
    sref,
    corner,
    cweight,
    part,
    fields,
    blocked,
    sample,
    sample_in,
    solid_x,
    solid_y,
    solid_d,
    part_in,
    fields_in,
    rows,
    rows_in,
    rows_d,
    rolled,
    posts,
    edges,
    in_sem,
    s_send,
    s_recv,
    h_send,
    h_recv,
):
    p = lax.axis_index("gx")
    q = lax.axis_index("gy")
    px = [lax.rem(p + n_gx + a, n_gx) for a in (-1, 0, 1)]
    qy = [lax.rem(q + n_gy + b, n_gy) for b in (-1, 0, 1)]
    around = [lax.rem(q + k, n_gy) for k in range(n_gy)]

    barrier = pltpu.get_barrier_semaphore()
    by_distance = sorted(range(n_gy), key=lambda k: -min(k, n_gy - k))
    targets = [(a, k) for a in (1, 0, -1) for k in by_distance if a or k]
    for a, k in targets:
        pl.semaphore_signal(
            barrier, inc=1, device_id=(px[a + 1], around[k]), device_id_type=MESH
        )

    loads = [
        pltpu.make_async_copy(src, dst, in_sem.at[k])
        for k, (src, dst) in enumerate(
            [
                (pop_h, pop),
                (relax_h, relax_s),
                (corner_h, corner),
                (cweight_h, cweight),
                (cell_h, cell),
                (normal_h, normal),
                (ref_h, sref),
                (solid_h, solid),
            ]
        )
    ]
    for copy in loads:
        copy.start()
    row_id = lax.broadcasted_iota(I32, (8, 128), 0)

    for copy in loads[:7]:
        copy.wait()

    cells = cell[0]
    live = lax.broadcasted_iota(I32, (1, 512), 1) < count_s[0, 0]
    refs = sref[0]
    first = jnp.where(live, (refs & 63) + 1, 0)
    second = jnp.where(live, (refs >> 6) * 8 + normal[0], 0)
    rows16 = lax.broadcasted_iota(I32, (16, 512), 0) == (cells >> 7)
    left = jnp.concatenate(
        [jnp.where(rows16, first, 0), jnp.where(rows16, second, 0)], axis=0
    ).astype(F32).astype(jnp.bfloat16)
    right = jnp.where(
        lax.broadcasted_iota(I32, (128, 512), 0) == (cells & 127), 1.0, 0.0
    ).astype(jnp.bfloat16)
    code = lax.dot_general(
        left, right, (((1,), (1,)), ((), ())), preferred_element_type=F32
    ).astype(I32)
    slot = code[0:16]
    owner = code[16:32]
    use = jnp.where(slot > 0, (owner >> 3) * 64 + slot, 0).astype(F32)
    axes = ((owner & 7) >> 1).astype(F32)
    for x in range(2):
        fields[4, x] = use[8 * x : 8 * x + 8]
        fields[5, x] = axes[8 * x : 8 * x + 8]

    vel = []
    for x in range(2):
        f = [pop[i, x] * weight[i] for i in range(27)]
        for axis in (2, 1, 0):
            f = along(f, axis, to_moments)
        rho = f[0]
        inv = 1.0 / rho
        u = [f[9] * inv, f[3] * inv, f[1] * inv]
        vel.append(u)
        fields[0, x] = rho
        for k in range(3):
            fields[k + 1, x] = u[k]
        balance = equilibrium_moments(rho, u)
        for m in range(27):
            off = f[m] if balance[m] is None else f[m] - balance[m]
            f[m] = off * (1.0 - relax_s[m])
        for axis in (2, 1, 0):
            f = along(f, axis, from_moments)
        for i, e in enumerate(steps):
            part[i, x] = f[i] * float(np.prod([1.5 if v == 0 else 3.0 for v in e]))

    for j in range(4):
        total = [jnp.zeros((8, 128), F32) for _ in range(3)]
        lanes = slice(128 * j, 128 * (j + 1))
        for k in range(8):
            where = jnp.broadcast_to(corner[0, 0, k : k + 1, lanes], (8, 128))
            share = jnp.broadcast_to(cweight[0, 0, k : k + 1, lanes], (8, 128))
            lane = where & 127
            mine = jnp.where((where >> 7) & 7 == row_id, share, 0.0)
            upper = where >= 1024
            for n in range(3):
                got = jnp.where(upper, lane_gather(vel[1][n], lane), lane_gather(vel[0][n], lane))
                total[n] = total[n] + mine * got
        for n in range(3):
            summed = jnp.sum(total[n], axis=0, keepdims=True)
            sample[3 * j + n] = summed
            if j == 0:
                sample[12 + n] = summed

    for m, b in enumerate((1, -1)):
        near = slice(7, 8) if b == 1 else slice(0, 1)
        base = 42 * m
        for c in (-1, 0, 1):
            for s, (a, x) in enumerate(((0, 0), (0, 1), (1, 0), (-1, 1))):
                rows[base + 4 * (c + 1) + s] = part[index_of[a, b, c], x, near]
            for n, (a, x) in enumerate(((1, 1), (-1, 0))):
                rows[base + 24 + 9 * n + c + 1] = part[index_of[a, b, c], x, near]
        for k in range(6):
            for x in range(2):
                value = fields[k, x, near]
                rows[base + 12 + 6 * x + k] = value
                rows[base + 27 + 9 * (1 - x) + k] = value

    par = lax.rem(q, 2)

    def window(d):
        return 3 * lax.div(lax.rem(d + n_gy - 1, n_gy), 2)

    mine = window(q)
    for r in range(6):
        sample_in[(n_gy + q) * 6 + r] = sample[mine + r]

    loads[7].wait()
    pl.semaphore_wait(barrier, len(targets))

    def send(src, dst, send_sem, recv_sem, peer):
        copy = pltpu.make_async_remote_copy(
            src_ref=src, dst_ref=dst, send_sem=send_sem, recv_sem=recv_sem,
            device_id=peer, device_id_type=MESH,
        )
        copy.start()
        return copy

    def send_samples(a):
        return [
            send(
                sample.at[pl.ds(window(around[k]), 6)],
                sample_in.at[pl.ds(((1 - a) * n_gy + q) * 6, 6)],
                s_send.at[t],
                s_recv.at[(1 - a) * n_gy + q],
                (px[a + 1], around[k]),
            )
            for t, (b, k) in enumerate(targets)
            if b == a
        ]

    def send_side(n):
        a = 1 - 2 * n
        x = 1 - n
        to = px[a + 1]
        halo = []
        for m, b in enumerate((1, -1)):
            halo.append(
                (rows.at[pl.ds(42 * m + 24 + 9 * n, 9)], rows_d.at[pl.ds((2 * n + m) * 9, 9)], (to, qy[b + 1]))
            )
        halo.append((fields.at[:, x], fields_in.at[n], (to, q)))
        halo.append((part.at[pl.ds(18 - 18 * n, 9), x], part_in.at[n], (to, q)))
        halo.append((solid.at[x], solid_x.at[n], (to, q)))
        for m, b in enumerate((1, -1)):
            halo.append((solid.at[x], solid_d.at[n, m], (to, qy[b + 1])))
        return [
            send(src, dst, h_send.at[7 * n + k], h_recv.at[7 * n + k], peer)
            for k, (src, dst, peer) in enumerate(halo)
        ]

    def send_row():
        halo = []
        for m, b in enumerate((1, -1)):
            to = (p, qy[b + 1])
            halo.append((rows.at[pl.ds(42 * m, 24)], rows_in.at[pl.ds(24 * m, 24)], to))
            halo.append((solid, solid_y.at[m], to))
        return [
            send(src, dst, h_send.at[14 + k], h_recv.at[14 + k], peer)
            for k, (src, dst, peer) in enumerate(halo)
        ]

    sent = send_samples(1)
    up = send_side(0)
    sent = sent + send_samples(0)
    row = send_row()
    sent = sent + send_samples(-1)
    down = send_side(1)

    def received(g, k):
        pltpu.make_async_remote_copy(
            src_ref=sample.at[pl.ds(0, 6)],
            dst_ref=sample_in.at[pl.ds((g * n_gy + around[k]) * 6, 6)],
            send_sem=s_send.at[0],
            recv_sem=s_recv.at[g * n_gy + around[k]],
            device_id=(p, around[k]),
            device_id_type=MESH,
        ).wait_recv()

    chunk = [0, 1 - par, 1]
    half = [1 - par, par, 1 - par]

    def table(g, t, k, n):
        return line(sample_in, (g * n_gy + around[k]) * 6 + 3 * chunk[t] + n)

    def wall_velocity(use, axis, u, tables, lanes):
        use = use.astype(I32)
        spot = use - 1
        who = spot >> 6
        lane = (spot & 63) + lanes
        picked = [jnp.zeros((8, 128), F32) for _ in range(3)]
        for k in reversed(by_distance):
            here = who == around[k]
            for n in range(3):
                picked[n] = jnp.where(here, lane_gather(tables(k, n), lane), picked[n])
        return [
            jnp.where(use > 0, jnp.where(axis == float(n), 0.0, wall_ratio * picked[n]), u[n])
            for n in range(3)
        ]

    def base_of(rho, u):
        return rho - 1.5 * rho * (u[0] * u[0] + u[1] * u[1] + u[2] * u[2])

    for k in range(1, n_gy):
        received(1, k)
    for x in range(2):
        rho = fields[0, x]
        u = wall_velocity(
            fields[4, x], fields[5, x], [fields[1 + n, x] for n in range(3)],
            lambda k, n: table(1, 1, k, n), half[1] * 64,
        )
        base = base_of(rho, u)
        for i in range(13, 27):
            along_e = total_of(u, steps[i])
            if along_e is None:
                posts[i, x] = part[i, x] + base
                continue
            linear = 3.0 * rho * along_e
            even = base + 1.5 * along_e * linear
            posts[i, x] = part[i, x] + (even + linear)
            posts[26 - i, x] = part[26 - i, x] + (even - linear)
    for i, (a, b, c) in enumerate(steps):
        for x in range(2):
            if 0 <= x + a <= 1:
                rolled[i, x] = shifted(posts[i, x], b, c)

    def side(n):
        a = 1 - 2 * n
        rho = fields_in[n, 0]
        u = wall_velocity(
            fields_in[n, 4], fields_in[n, 5], [fields_in[n, 1 + k] for k in range(3)],
            lambda k, m: table(2 * n, 1, k, m), half[1] * 64,
        )
        base = base_of(rho, u)
        for s, (b, c) in enumerate((b, c) for b in (-1, 0, 1) for c in (-1, 0, 1)):
            along_e = total_of(u, (a, b, c))
            linear = 3.0 * rho * along_e
            value = part_in[n, s] + (base + linear + 1.5 * along_e * linear)
            rolled[index_of[a, b, c], 1 - n] = shifted(value, b, c)

    for copy in down:
        copy.wait_recv()
    for k in range(n_gy):
        received(2, k)
    side(1)
    for copy in row + up:
        copy.wait_recv()

    flags = [solid_x[0], solid[0], solid[1], solid_x[1]]
    for xx in range(4):
        for b in (-1, 0, 1):
            plane = flags[xx]
            if b:
                m = 0 if b == 1 else 1
                near = 7 if b == 1 else 0
                if xx in (1, 2):
                    edge = row_of(solid_y, (m, xx - 1), near)
                else:
                    edge = row_of(solid_d, (0 if xx == 0 else 1, m), near)
                plane = pltpu.roll(plane, b % 8, 0)
                plane = jnp.where(row_id == (0 if b == 1 else 7), edge, plane)
            for c in (-1, 0, 1):
                blocked[xx, 3 * (b + 1) + c + 1] = shifted(plane, 0, c)

    at = [row_id == s for s in range(8)]

    def gather_rows(entries):
        value = None
        for s, piece in entries:
            value = piece if value is None else jnp.where(at[s], piece, value)
        return value

    def field_row(k):
        entries = []
        for m in range(2):
            entries.append((4 * m, line(rows_d, m * 9 + 3 + k)))
            entries.append((4 * m + 1, line(rows_in, m * 24 + 12 + k)))
            entries.append((4 * m + 2, line(rows_in, m * 24 + 18 + k)))
            entries.append((4 * m + 3, line(rows_d, (2 + m) * 9 + 3 + k)))
        return gather_rows(entries)

    edge_fields = [field_row(k) for k in range(6)]
    edge_part = {}
    for a in (-1, 0, 1):
        for c in (-1, 0, 1):
            entries = []
            for m in range(2):
                base = m * 24 + 4 * (c + 1)
                if a == 0:
                    entries.append((4 * m + 1, line(rows_in, base)))
                    entries.append((4 * m + 2, line(rows_in, base + 1)))
                elif a == 1:
                    entries.append((4 * m, line(rows_d, m * 9 + c + 1)))
                    entries.append((4 * m + 1, line(rows_in, base + 2)))
                else:
                    entries.append((4 * m + 2, line(rows_in, base + 3)))
                    entries.append((4 * m + 3, line(rows_d, (2 + m) * 9 + c + 1)))
            edge_part[a, c] = gather_rows(entries)

    for k in range(n_gy):
        received(0, k)
    side(0)

    lower = row_id < 4
    across = row_id & 3

    def edge_table(k, n):
        value = table(1, 0, k, n)
        value = jnp.where(lower, value, table(1, 2, k, n))
        for g, s in ((2, 3), (0, 0)):
            value = jnp.where(
                across == s, jnp.where(lower, table(g, 0, k, n), table(g, 2, k, n)), value
            )
        return value

    rho = edge_fields[0]
    u = wall_velocity(
        edge_fields[4], edge_fields[5], edge_fields[1:4], edge_table, (1 - par) * 64
    )
    base = base_of(rho, u)
    u = [u[0], jnp.where(lower, u[1], -u[1]), u[2]]
    for s, (a, c) in enumerate((a, c) for a in (-1, 0, 1) for c in (-1, 0, 1)):
        along_e = total_of(u, (a, 1, c))
        linear = 3.0 * rho * along_e
        value = edge_part[a, c] + (base + linear + 1.5 * along_e * linear)
        edges[s] = shifted(value, 0, c)

    for i, (a, b, c) in enumerate(steps):
        for x in range(2):
            xx = x - a
            if 0 <= xx <= 1:
                value = rolled[i, xx]
            else:
                value = rolled[i, 1 if a == 1 else 0]
            if b:
                m = 0 if b == 1 else 1
                edge = row_of(edges, (3 * (a + 1) + c + 1,), 4 * m + xx + 1)
                value = jnp.where(row_id == (0 if b == 1 else 7), edge, value)
            wall = blocked[xx + 1, 3 * (b + 1) + c + 1]
            out[i, x] = jnp.where(wall != 0, posts[26 - i, x], value)

    for copy in sent + up + row + down:
        copy.wait_send()


def local(*args):
    n_gx, n_gy = lax.axis_size("gx"), lax.axis_size("gy")
    hbm = pl.BlockSpec(memory_space=pl.ANY)
    smem = pl.BlockSpec(memory_space=pltpu.SMEM)
    vmem = pltpu.VMEM
    dma = pltpu.SemaphoreType.DMA
    args = [
        a if k == 5 else pltpu.with_memory_space_constraint(a, pltpu.HBM)
        for k, a in enumerate(args)
    ]
    return pl.pallas_call(
        lambda *refs: body(n_gx, n_gy, *refs),
        name="lattice_step",
        out_shape=vmem((27, 2, 8, 128), F32),
        in_specs=[hbm, hbm, hbm, hbm, hbm, smem, hbm, hbm, hbm],
        out_specs=pl.BlockSpec(memory_space=pltpu.VMEM),
        scratch_shapes=[
            pltpu.SMEM((27,), F32),
            vmem((27, 2, 8, 128), F32),
            vmem((2, 8, 128), I32),
            vmem((1, 1, 512), I32),
            vmem((1, 1, 512), I32),
            vmem((1, 1, 512), I32),
            vmem((1, 1, 8, 512), I32),
            vmem((1, 1, 8, 512), F32),
            vmem((27, 2, 8, 128), F32),
            vmem((6, 2, 8, 128), F32),
            vmem((4, 9, 8, 128), I32),
            vmem((15, 1, 128), F32),
            vmem((3 * n_gy * 6, 1, 128), F32),
            vmem((2, 8, 128), I32),
            vmem((2, 2, 8, 128), I32),
            vmem((2, 2, 8, 128), I32),
            vmem((2, 9, 8, 128), F32),
            vmem((2, 6, 8, 128), F32),
            vmem((84, 1, 128), F32),
            vmem((48, 1, 128), F32),
            vmem((36, 1, 128), F32),
            vmem((27, 2, 8, 128), F32),
            vmem((27, 2, 8, 128), F32),
            vmem((9, 8, 128), F32),
            dma((8,)),
            dma((3 * n_gy - 1,)),
            dma((3 * n_gy,)),
            dma((18,)),
            dma((18,)),
        ],
        compiler_params=pltpu.CompilerParams(
            collective_id=0, has_side_effects=True, vmem_limit_bytes=16 << 20
        ),
    )(*args)


def solution(mesh):
    return jax.shard_map(
        local,
        mesh=mesh,
        in_specs=(
            P(None, "gx", "gy", None),
            P(),
            P("gx", "gy", None),
            P("gx", "gy", None),
            P("gx", "gy", None),
            P("gx", "gy"),
            P("gx", "gy", None),
            P("gx", "gy", None, None),
            P("gx", "gy", None, None),
        ),
        out_specs=P(None, "gx", "gy", None),
        check_vma=False,
    )
```

time: 36.5 us -> 30.6 us (0.84)
  Pallas kernels: 34 us -> 29 us
  local copies, waits for them, and re-layouts: 1.64 us -> 0.69 us
    pallas_call x1, Pallas kernels: 34 us -> 29 us  [local(): pl.pallas_call(lambda *refs: body(n_gx, n_gy, *refs), name='lattice_step'...]
    unnamed x1, local copies, waits for them, and re-layouts: 1.64 us -> 0.69 us
where the time goes in v2:
time: 30.6 us; the launch traced here: 30.4 us
  Pallas kernels  29 us (95%)
  local copies, waits for them, and re-layouts  0.69 us (2%)
  between operations  0.66 us (2%)
    pallas_call x1, Pallas kernels, local(): pl.pallas_call(lambda *refs: body(n_gx, n_gy, *refs), name='lattice_step'...  29 us
    unnamed x1, local copies, waits for them, and re-layouts  0.69 us

profile of v2, /device:TPU:1, one launch (start us, length us, event | category | flops | bytes accessed | tf_op | source)
XLA Modules:
  0.0 30.4 jit_solution(12267088027327987676)
XLA Ops:
  0.7 29.0 %lattice_step.1 = f32[27,2,8,128]{3,2,1,0:T(8,128)S(1)} custom-call(f32[27,2,8,128]{3,2,1,0:T(8,128)} %refs_0_.1, f32[27]{0:T(128)} %refs_1_.1, s32[2,8,128]{2,1,0:T(8,128)} %refs_2_.1, s32[1,1,512]{2,1,0:T(1,128)} %refs_3_.1, s32[1,1,512]{2,1,0:T(1,128)} %refs_4_.1, s32[1,1]{1,0:T(1,128)S(6)} %copy.12.refs_5_, s32[1,1,512]{2,1,0:T(1,128)} %refs_6_.1, ...), custom_call_target="tpu_custom_call" | custom-call | tf_op jit(solution)/shard_map/lattice_step/pallas_call | solution.py:502
  29.7 0.7 %copy.11 = f32[27,2,8,128]{3,2,1,0:T(8,128)} copy(f32[27,2,8,128]{3,2,1,0:T(8,128)S(1)} %lattice_step.1) | data formatting | bytes 442368

commit v3 on v2

v3 whole, which is shorter than its diff:
```python
import jax
import jax.numpy as jnp
import numpy as np
from jax import lax
from jax.experimental import pallas as pl
from jax.experimental.pallas import tpu as pltpu
from jax.sharding import PartitionSpec as P

MESH = pl.DeviceIdType.MESH
wall_ratio = (1.0 / 9.0) ** (1.0 / 7.0)
steps = [(a, b, c) for a in (-1, 0, 1) for b in (-1, 0, 1) for c in (-1, 0, 1)]
index_of = {e: i for i, e in enumerate(steps)}
weight = [float(np.prod([2.0 / 3.0 if v == 0 else 1.0 / 6.0 for v in e])) for e in steps]
F32 = jnp.float32
I32 = jnp.int32


def along(values, axis, combine):
    stride = (9, 3, 1)[axis]
    out = list(values)
    for i in range(27):
        if i // stride % 3 == 0:
            out[i], out[i + stride], out[i + 2 * stride] = combine(
                values[i], values[i + stride], values[i + 2 * stride]
            )
    return out


def to_moments(lo, mid, hi):
    both = hi + lo
    return both + mid, hi - lo, both


def from_moments(zero, one, two):
    return two - one, zero - two, two + one


def equilibrium_moments(rho, vel):
    sq = [v * v for v in vel]
    third = 1.0 / 3.0
    out = []
    for powers in [(a, b, c) for a in range(3) for b in range(3) for c in range(3)]:
        odd = [k for k in range(3) if powers[k] == 1]
        even = [k for k in range(3) if powers[k] == 2]
        scale = third ** len(even)
        if len(odd) == 3:
            out.append(None)
        elif len(odd) == 2:
            out.append(rho * (vel[odd[0]] * vel[odd[1]] * scale))
        elif len(odd) == 1:
            out.append(rho * (vel[odd[0]] * scale))
        elif not even:
            out.append(rho)
        else:
            total = sq[even[0]]
            for k in even[1:]:
                total = total + sq[k]
            out.append(rho * (scale + 3.0 * scale * total))
    return out


def shifted(value, b, c):
    if c:
        value = pltpu.roll(value, c % 128, 1)
    if b:
        value = pltpu.roll(value, b % 8, 0)
    return value


def lane_gather(table, index):
    return jnp.take_along_axis(table, index, axis=1, mode="promise_in_bounds")


def row_of(ref, lead, row):
    return jnp.broadcast_to(ref[lead + (slice(row, row + 1), slice(None))], (8, 128))


def line(ref, row):
    return jnp.broadcast_to(ref[row], (8, 128))


def total_of(u, e):
    total = None
    for n in range(3):
        if e[n]:
            term = u[n] if e[n] > 0 else -u[n]
            total = term if total is None else total + term
    return total


def body(
    n_gx,
    n_gy,
    pop_h,
    relax_h,
    solid_h,
    cell_h,
    normal_h,
    count_s,
    ref_h,
    corner_h,
    cweight_h,
    out,
    relax_s,
    pop,
    solid,
    cell,
    normal,
    sref,
    corner,
    cweight,
    part,
    fields,
    blocked,
    sample,
    sample_in,
    solid_x,
    solid_y,
    solid_d,
    part_in,
    fields_in,
    rows,
    rows_in,
    rows_d,
    rolled,
    posts,
    edges,
    in_sem,
    tally,
    s_send,
    s_recv,
    h_send,
    h_recv,
    ready,
):
    p = lax.axis_index("gx")
    q = lax.axis_index("gy")
    px = [lax.rem(p + n_gx + a, n_gx) for a in (-1, 0, 1)]
    qy = [lax.rem(q + n_gy + b, n_gy) for b in (-1, 0, 1)]
    around = [lax.rem(q + k, n_gy) for k in range(n_gy)]

    loads = [
        pltpu.make_async_copy(src, dst, in_sem.at[k])
        for k, (src, dst) in enumerate(
            [
                (pop_h, pop),
                (corner_h, corner),
                (cweight_h, cweight),
                (relax_h, relax_s),
                (cell_h, cell),
                (normal_h, normal),
                (ref_h, sref),
                (solid_h, solid),
            ]
        )
    ]
    for copy in loads:
        copy.start()

    barrier = pltpu.get_barrier_semaphore()
    by_distance = sorted(range(n_gy), key=lambda k: -min(k, n_gy - k))
    targets = [(a, k) for a in (1, 0, -1) for k in by_distance if a or k]
    greeted = [(a, k) for a in (-1, 0) for k in by_distance if a or k]
    for a, k in greeted:
        pl.semaphore_signal(
            barrier, inc=1, device_id=(px[a + 1], around[k]), device_id_type=MESH
        )
    row_id = lax.broadcasted_iota(I32, (8, 128), 0)

    vel = []
    for copy in loads[:3]:
        copy.wait()
    for x in range(2):
        f = [pop[i, x] * weight[i] for i in range(27)]
        for axis in (2, 1, 0):
            f = along(f, axis, to_moments)
        rho = f[0]
        inv = 1.0 / rho
        u = [f[9] * inv, f[3] * inv, f[1] * inv]
        vel.append(u)
        fields[0, x] = rho
        for k in range(3):
            fields[k + 1, x] = u[k]
        for m in range(27):
            part[m, x] = f[m]

    for j in range(4):
        total = [jnp.zeros((8, 128), F32) for _ in range(3)]
        lanes = slice(128 * j, 128 * (j + 1))
        for k in range(8):
            where = jnp.broadcast_to(corner[0, 0, k : k + 1, lanes], (8, 128))
            share = jnp.broadcast_to(cweight[0, 0, k : k + 1, lanes], (8, 128))
            lane = where & 127
            mine = jnp.where((where >> 7) & 7 == row_id, share, 0.0)
            upper = where >= 1024
            for n in range(3):
                got = jnp.where(upper, lane_gather(vel[1][n], lane), lane_gather(vel[0][n], lane))
                total[n] = total[n] + mine * got
        for n in range(3):
            summed = jnp.sum(total[n], axis=0, keepdims=True)
            sample[3 * j + n] = summed
            if j == 0:
                sample[12 + n] = summed

    par = lax.rem(q, 2)

    def window(d):
        return 3 * lax.div(lax.rem(d + n_gy - 1, n_gy), 2)

    mine = window(q)
    for r in range(6):
        sample_in[(n_gy + q) * 6 + r] = sample[mine + r]

    def send(src, dst, send_sem, recv_sem, peer):
        pltpu.make_async_remote_copy(
            src_ref=src, dst_ref=dst, send_sem=send_sem, recv_sem=recv_sem,
            device_id=peer, device_id_type=MESH,
        ).start()

    def send_samples(a):
        for b, k in targets:
            if b == a:
                send(
                    sample.at[pl.ds(window(around[k]), 6)],
                    sample_in.at[pl.ds(((1 - a) * n_gy + q) * 6, 6)],
                    s_send,
                    s_recv.at[1 - a],
                    (px[a + 1], around[k]),
                )

    def send_side(n):
        a = 1 - 2 * n
        x = 1 - n
        to = px[a + 1]
        halo = []
        for m, b in enumerate((1, -1)):
            halo.append(
                (rows.at[pl.ds(42 * m + 24 + 9 * n, 9)], rows_d.at[pl.ds((2 * n + m) * 9, 9)], (to, qy[b + 1]))
            )
        halo.append((fields.at[:, x], fields_in.at[n], (to, q)))
        halo.append((part.at[pl.ds(18 - 18 * n, 9), x], part_in.at[n], (to, q)))
        halo.append((solid.at[x], solid_x.at[n], (to, q)))
        for m, b in enumerate((1, -1)):
            halo.append((solid.at[x], solid_d.at[n, m], (to, qy[b + 1])))
        for src, dst, peer in halo:
            send(src, dst, h_send, h_recv.at[n], peer)

    def send_row():
        for m, b in enumerate((1, -1)):
            to = (p, qy[b + 1])
            send(rows.at[pl.ds(42 * m, 24)], rows_in.at[pl.ds(24 * m, 24)], h_send, h_recv.at[2], to)
            send(solid, solid_y.at[m], h_send, h_recv.at[2], to)

    def arrived(sem, lines):
        span = tally.at[pl.ds(0, lines)]
        pltpu.make_async_copy(span, span, sem).wait()

    side_lines = 2 * 9 + 48 + 72 + 24
    row_lines = 2 * (24 + 16)

    pl.semaphore_wait(barrier, len(greeted))
    send_samples(1)
    for k in by_distance:
        pl.semaphore_signal(
            ready, inc=1, device_id=(px[2], around[k]), device_id_type=MESH
        )

    for copy in loads[4:]:
        copy.wait()
    cells = cell[0]
    live = lax.broadcasted_iota(I32, (1, 512), 1) < count_s[0, 0]
    refs = sref[0]
    first = jnp.where(live, (refs & 63) + 1, 0)
    second = jnp.where(live, (refs >> 6) * 8 + normal[0], 0)
    rows16 = lax.broadcasted_iota(I32, (16, 512), 0) == (cells >> 7)
    left = jnp.concatenate(
        [jnp.where(rows16, first, 0), jnp.where(rows16, second, 0)], axis=0
    ).astype(F32).astype(jnp.bfloat16)
    right = jnp.where(
        lax.broadcasted_iota(I32, (128, 512), 0) == (cells & 127), 1.0, 0.0
    ).astype(jnp.bfloat16)
    code = lax.dot_general(
        left, right, (((1,), (1,)), ((), ())), preferred_element_type=F32
    ).astype(I32)
    slot = code[0:16]
    owner = code[16:32]
    use = jnp.where(slot > 0, (owner >> 3) * 64 + slot, 0).astype(F32)
    axes = ((owner & 7) >> 1).astype(F32)
    for x in range(2):
        fields[4, x] = use[8 * x : 8 * x + 8]
        fields[5, x] = axes[8 * x : 8 * x + 8]

    loads[3].wait()
    for x in range(2):
        f = [part[m, x] for m in range(27)]
        balance = equilibrium_moments(fields[0, x], [fields[1 + k, x] for k in range(3)])
        for m in range(27):
            off = f[m] if balance[m] is None else f[m] - balance[m]
            f[m] = off * (1.0 - relax_s[m])
        for axis in (2, 1, 0):
            f = along(f, axis, from_moments)
        for i, e in enumerate(steps):
            part[i, x] = f[i] * float(np.prod([1.5 if v == 0 else 3.0 for v in e]))

    for m, b in enumerate((1, -1)):
        near = slice(7, 8) if b == 1 else slice(0, 1)
        base = 42 * m
        for c in (-1, 0, 1):
            for s, (a, x) in enumerate(((0, 0), (0, 1), (1, 0), (-1, 1))):
                rows[base + 4 * (c + 1) + s] = part[index_of[a, b, c], x, near]
            for n, (a, x) in enumerate(((1, 1), (-1, 0))):
                rows[base + 24 + 9 * n + c + 1] = part[index_of[a, b, c], x, near]
        for k in range(6):
            for x in range(2):
                value = fields[k, x, near]
                rows[base + 12 + 6 * x + k] = value
                rows[base + 27 + 9 * (1 - x) + k] = value

    send_side(0)
    send_samples(0)
    send_row()
    pl.semaphore_wait(ready, n_gy)
    send_samples(-1)
    send_side(1)

    chunk = [0, 1 - par, 1]
    half = [1 - par, par, 1 - par]

    def table(g, t, k, n):
        return line(sample_in, (g * n_gy + around[k]) * 6 + 3 * chunk[t] + n)

    def wall_velocity(use, axis, u, tables, lanes):
        use = use.astype(I32)
        spot = use - 1
        who = spot >> 6
        lane = (spot & 63) + lanes
        picked = [jnp.zeros((8, 128), F32) for _ in range(3)]
        for k in reversed(by_distance):
            here = who == around[k]
            for n in range(3):
                picked[n] = jnp.where(here, lane_gather(tables(k, n), lane), picked[n])
        return [
            jnp.where(use > 0, jnp.where(axis == float(n), 0.0, wall_ratio * picked[n]), u[n])
            for n in range(3)
        ]

    def base_of(rho, u):
        return rho - 1.5 * rho * (u[0] * u[0] + u[1] * u[1] + u[2] * u[2])

    arrived(s_recv.at[1], (n_gy - 1) * 6)
    for x in range(2):
        rho = fields[0, x]
        u = wall_velocity(
            fields[4, x], fields[5, x], [fields[1 + n, x] for n in range(3)],
            lambda k, n: table(1, 1, k, n), half[1] * 64,
        )
        base = base_of(rho, u)
        for i in range(13, 27):
            along_e = total_of(u, steps[i])
            if along_e is None:
                posts[i, x] = part[i, x] + base
                continue
            linear = 3.0 * rho * along_e
            even = base + 1.5 * along_e * linear
            posts[i, x] = part[i, x] + (even + linear)
            posts[26 - i, x] = part[26 - i, x] + (even - linear)
    for i, (a, b, c) in enumerate(steps):
        for x in range(2):
            if 0 <= x + a <= 1:
                rolled[i, x] = shifted(posts[i, x], b, c)

    def side(n):
        a = 1 - 2 * n
        rho = fields_in[n, 0]
        u = wall_velocity(
            fields_in[n, 4], fields_in[n, 5], [fields_in[n, 1 + k] for k in range(3)],
            lambda k, m: table(2 * n, 1, k, m), half[1] * 64,
        )
        base = base_of(rho, u)
        for s, (b, c) in enumerate((b, c) for b in (-1, 0, 1) for c in (-1, 0, 1)):
            along_e = total_of(u, (a, b, c))
            linear = 3.0 * rho * along_e
            value = part_in[n, s] + (base + linear + 1.5 * along_e * linear)
            rolled[index_of[a, b, c], 1 - n] = shifted(value, b, c)

    def block_plane(xx, plane):
        for b in (-1, 0, 1):
            moved = plane
            if b:
                m = 0 if b == 1 else 1
                near = 7 if b == 1 else 0
                if xx in (1, 2):
                    edge = row_of(solid_y, (m, xx - 1), near)
                else:
                    edge = row_of(solid_d, (0 if xx == 0 else 1, m), near)
                moved = pltpu.roll(plane, b % 8, 0)
                moved = jnp.where(row_id == (0 if b == 1 else 7), edge, moved)
            for c in (-1, 0, 1):
                blocked[xx, 3 * (b + 1) + c + 1] = shifted(moved, 0, c)

    at = [row_id == s for s in range(8)]
    lower = row_id < 4
    across = row_id & 3

    def gather_rows(entries):
        value = None
        for s, piece in entries:
            value = piece if value is None else jnp.where(at[s], piece, value)
        return value

    def field_row(k, near):
        entries = []
        for m in range(2):
            if near:
                entries.append((4 * m + 1, line(rows_in, m * 24 + 12 + k)))
                entries.append((4 * m + 2, line(rows_in, m * 24 + 18 + k)))
                entries.append((4 * m + 3, line(rows_d, (2 + m) * 9 + 3 + k)))
            else:
                entries.append((4 * m, line(rows_d, m * 9 + 3 + k)))
        return gather_rows(entries)

    def part_row(a, c, near):
        entries = []
        for m in range(2):
            base = m * 24 + 4 * (c + 1)
            if not near:
                entries.append((4 * m, line(rows_d, m * 9 + c + 1)))
            elif a == 0:
                entries.append((4 * m + 1, line(rows_in, base)))
                entries.append((4 * m + 2, line(rows_in, base + 1)))
            elif a == 1:
                entries.append((4 * m + 1, line(rows_in, base + 2)))
            else:
                entries.append((4 * m + 2, line(rows_in, base + 3)))
                entries.append((4 * m + 3, line(rows_d, (2 + m) * 9 + c + 1)))
        return gather_rows(entries)

    def table_near(k, n):
        value = jnp.where(lower, table(1, 0, k, n), table(1, 2, k, n))
        other = jnp.where(lower, table(2, 0, k, n), table(2, 2, k, n))
        return jnp.where(across == 3, other, value)

    def table_far(k, n):
        return jnp.where(lower, table(0, 0, k, n), table(0, 2, k, n))

    def edge_rows(found, parts, tables, where):
        rho = found[0]
        u = wall_velocity(found[4], found[5], found[1:4], tables, (1 - par) * 64)
        base = base_of(rho, u)
        u = [u[0], jnp.where(lower, u[1], -u[1]), u[2]]
        for (a, c), piece in parts.items():
            along_e = total_of(u, (a, 1, c))
            linear = 3.0 * rho * along_e
            value = piece + (base + linear + 1.5 * along_e * linear)
            edges[where + 3 * (a + 1) + c + 1] = shifted(value, 0, c)

    def finish(far):
        for i, (a, b, c) in enumerate(steps):
            for x in range(2):
                xx = x - a
                if (xx == -1) != far:
                    continue
                value = rolled[i, xx if 0 <= xx <= 1 else 1 if a == 1 else 0]
                if b:
                    m = 0 if b == 1 else 1
                    s = (9 if far else 0) + 3 * (a + 1) + c + 1
                    edge = row_of(edges, (s,), 4 * m + xx + 1)
                    value = jnp.where(row_id == (0 if b == 1 else 7), edge, value)
                wall = blocked[xx + 1, 3 * (b + 1) + c + 1]
                out[i, x] = jnp.where(wall != 0, posts[26 - i, x], value)

    arrived(h_recv.at[2], row_lines)
    arrived(h_recv.at[1], side_lines)
    for xx, plane in ((1, solid[0]), (2, solid[1]), (3, solid_x[1])):
        block_plane(xx, plane)
    found = [field_row(k, True) for k in range(6)]
    parts = {(a, c): part_row(a, c, True) for a in (-1, 0, 1) for c in (-1, 0, 1)}
    arrived(s_recv.at[2], n_gy * 6)
    side(1)
    edge_rows(found, parts, table_near, 0)
    finish(False)

    arrived(h_recv.at[0], side_lines)
    block_plane(0, solid_x[0])
    found = [field_row(k, False) for k in range(6)]
    parts = {(1, c): part_row(1, c, False) for c in (-1, 0, 1)}
    arrived(s_recv.at[0], n_gy * 6)
    side(0)
    edge_rows(found, parts, table_far, 9)
    finish(True)

    arrived(s_send, len(targets) * 6)
    arrived(h_send, 2 * side_lines + row_lines)


def local(*args):
    n_gx, n_gy = lax.axis_size("gx"), lax.axis_size("gy")
    hbm = pl.BlockSpec(memory_space=pl.ANY)
    smem = pl.BlockSpec(memory_space=pltpu.SMEM)
    vmem = pltpu.VMEM
    dma = pltpu.SemaphoreType.DMA
    args = [
        a if k == 5 else pltpu.with_memory_space_constraint(a, pltpu.HBM)
        for k, a in enumerate(args)
    ]
    return pl.pallas_call(
        lambda *refs: body(n_gx, n_gy, *refs),
        name="lattice_step",
        out_shape=vmem((27, 2, 8, 128), F32),
        in_specs=[hbm, hbm, hbm, hbm, hbm, smem, hbm, hbm, hbm],
        out_specs=pl.BlockSpec(memory_space=pltpu.VMEM),
        scratch_shapes=[
            pltpu.SMEM((27,), F32),
            vmem((27, 2, 8, 128), F32),
            vmem((2, 8, 128), I32),
            vmem((1, 1, 512), I32),
            vmem((1, 1, 512), I32),
            vmem((1, 1, 512), I32),
            vmem((1, 1, 8, 512), I32),
            vmem((1, 1, 8, 512), F32),
            vmem((27, 2, 8, 128), F32),
            vmem((6, 2, 8, 128), F32),
            vmem((4, 9, 8, 128), I32),
            vmem((15, 1, 128), F32),
            vmem((3 * n_gy * 6, 1, 128), F32),
            vmem((2, 8, 128), I32),
            vmem((2, 2, 8, 128), I32),
            vmem((2, 2, 8, 128), I32),
            vmem((2, 9, 8, 128), F32),
            vmem((2, 6, 8, 128), F32),
            vmem((84, 1, 128), F32),
            vmem((48, 1, 128), F32),
            vmem((36, 1, 128), F32),
            vmem((27, 2, 8, 128), F32),
            vmem((27, 2, 8, 128), F32),
            vmem((18, 8, 128), F32),
            dma((8,)),
            vmem((404, 1, 128), F32),
            dma(()),
            dma((3,)),
            dma(()),
            dma((3,)),
            pltpu.SemaphoreType.REGULAR,
        ],
        compiler_params=pltpu.CompilerParams(
            collective_id=0, has_side_effects=True, vmem_limit_bytes=16 << 20
        ),
    )(*args)


def solution(mesh):
    return jax.shard_map(
        local,
        mesh=mesh,
        in_specs=(
            P(None, "gx", "gy", None),
            P(),
            P("gx", "gy", None),
            P("gx", "gy", None),
            P("gx", "gy", None),
            P("gx", "gy"),
            P("gx", "gy", None),
            P("gx", "gy", None, None),
            P("gx", "gy", None, None),
        ),
        out_specs=P(None, "gx", "gy", None),
        check_vma=False,
    )
```

time: 30.6 us -> 28.4 us (0.928)
  the two profiles are of different devices: /device:TPU:1 before, /device:TPU:8 now
where the time goes in v3:
time: 28.4 us; the launch traced here: 28.2 us
  Pallas kernels  26.9 us (95%)
  local copies, waits for them, and re-layouts  0.69 us (2%)
  between operations  0.66 us (2%)
    pallas_call x1, Pallas kernels, local(): pl.pallas_call(lambda *refs: body(n_gx, n_gy, *refs), name='lattice_step'...  26.9 us
    unnamed x1, local copies, waits for them, and re-layouts  0.69 us

profile of v3, /device:TPU:8, one launch (start us, length us, event | category | flops | bytes accessed | tf_op | source)
XLA Modules:
  0.0 28.2 jit_solution(8303917020299082315)
XLA Ops:
  0.7 26.9 %lattice_step.1 = f32[27,2,8,128]{3,2,1,0:T(8,128)S(1)} custom-call(f32[27,2,8,128]{3,2,1,0:T(8,128)} %refs_0_.1, f32[27]{0:T(128)} %refs_1_.1, s32[2,8,128]{2,1,0:T(8,128)} %refs_2_.1, s32[1,1,512]{2,1,0:T(1,128)} %refs_3_.1, s32[1,1,512]{2,1,0:T(1,128)} %refs_4_.1, s32[1,1]{1,0:T(1,128)S(6)} %copy.12.refs_5_, s32[1,1,512]{2,1,0:T(1,128)} %refs_6_.1, ...), custom_call_target="tpu_custom_call" | custom-call | tf_op jit(solution)/shard_map/lattice_step/pallas_call | solution.py:506
  27.5 0.7 %copy.11 = f32[27,2,8,128]{3,2,1,0:T(8,128)} copy(f32[27,2,8,128]{3,2,1,0:T(8,128)S(1)} %lattice_step.1) | data formatting | bytes 442368

commit v4 on v3

--- a/solution.py
+++ b/solution.py
@@ -132,8 +132,12 @@
     h_send,
     h_recv,
     ready,
+    whole,
 ):
     p = lax.axis_index("gx")
+    pop = pop_h
+    corner = corner_h
+    cweight = cweight_h
     q = lax.axis_index("gy")
     px = [lax.rem(p + n_gx + a, n_gx) for a in (-1, 0, 1)]
     qy = [lax.rem(q + n_gy + b, n_gy) for b in (-1, 0, 1)]
@@ -143,9 +147,6 @@
         pltpu.make_async_copy(src, dst, in_sem.at[k])
         for k, (src, dst) in enumerate(
             [
-                (pop_h, pop),
-                (corner_h, corner),
-                (cweight_h, cweight),
                 (relax_h, relax_s),
                 (cell_h, cell),
                 (normal_h, normal),
@@ -160,15 +161,14 @@
     barrier = pltpu.get_barrier_semaphore()
     by_distance = sorted(range(n_gy), key=lambda k: -min(k, n_gy - k))
     targets = [(a, k) for a in (1, 0, -1) for k in by_distance if a or k]
-    greeted = [(a, k) for a in (-1, 0) for k in by_distance if a or k]
-    for a, k in greeted:
+    for k in by_distance:
         pl.semaphore_signal(
-            barrier, inc=1, device_id=(px[a + 1], around[k]), device_id_type=MESH
+            barrier, inc=1, device_id=(px[0], around[k]), device_id_type=MESH
         )
     row_id = lax.broadcasted_iota(I32, (8, 128), 0)
 
     vel = []
-    for copy in loads[:3]:
+    for copy in loads[:0]:
         copy.wait()
     for x in range(2):
         f = [pop[i, x] * weight[i] for i in range(27)]
@@ -258,17 +258,17 @@
     side_lines = 2 * 9 + 48 + 72 + 24
     row_lines = 2 * (24 + 16)
 
-    pl.semaphore_wait(barrier, len(greeted))
+    pl.semaphore_wait(barrier, n_gy)
     send_samples(1)
     for k in by_distance:
         pl.semaphore_signal(
             ready, inc=1, device_id=(px[2], around[k]), device_id_type=MESH
         )
 
-    for copy in loads[4:]:
+    for copy in loads[1:]:
         copy.wait()
     cells = cell[0]
-    live = lax.broadcasted_iota(I32, (1, 512), 1) < count_s[0, 0]
+    live = count_s[...] > 0
     refs = sref[0]
     first = jnp.where(live, (refs & 63) + 1, 0)
     second = jnp.where(live, (refs >> 6) * 8 + normal[0], 0)
@@ -290,7 +290,7 @@
         fields[4, x] = use[8 * x : 8 * x + 8]
         fields[5, x] = axes[8 * x : 8 * x + 8]
 
-    loads[3].wait()
+    loads[0].wait()
     for x in range(2):
         f = [part[m, x] for m in range(27)]
         balance = equilibrium_moments(fields[0, x], [fields[1 + k, x] for k in range(3)])
@@ -317,9 +317,15 @@
                 rows[base + 27 + 9 * (1 - x) + k] = value
 
     send_side(0)
+    def greet():
+        pl.semaphore_wait(ready, n_gy)
+        pl.semaphore_signal(whole, inc=1, device_id=(px[0], q), device_id_type=MESH)
+
+    pl.when(p != 0)(greet)
+    pl.semaphore_wait(whole, 1)
     send_samples(0)
     send_row()
-    pl.semaphore_wait(ready, n_gy)
+    pl.when(p == 0)(greet)
     send_samples(-1)
     send_side(1)
 
@@ -493,6 +499,11 @@
     arrived(h_send, 2 * side_lines + row_lines)
 
 
+def mark_live(count, live):
+    spot = lax.broadcasted_iota(I32, live.shape, 1)
+    live[...] = jnp.where(spot < count[0, 0], 1, 0)
+
+
 def local(*args):
     n_gx, n_gy = lax.axis_size("gx"), lax.axis_size("gy")
     hbm = pl.BlockSpec(memory_space=pl.ANY)
@@ -500,14 +511,22 @@
     vmem = pltpu.VMEM
     dma = pltpu.SemaphoreType.DMA
     args = [
-        a if k == 5 else pltpu.with_memory_space_constraint(a, pltpu.HBM)
+        a if k in (0, 5, 7, 8) else pltpu.with_memory_space_constraint(a, pltpu.HBM)
         for k, a in enumerate(args)
     ]
+    args[5] = pl.pallas_call(
+        mark_live,
+        name="mark_live",
+        out_shape=vmem((1, 512), I32),
+        in_specs=[smem],
+        out_specs=pl.BlockSpec(memory_space=pltpu.VMEM),
+        cost_estimate=pl.CostEstimate(flops=100000000, bytes_accessed=1000, transcendentals=0),
+    )(args[5])
     return pl.pallas_call(
         lambda *refs: body(n_gx, n_gy, *refs),
         name="lattice_step",
         out_shape=vmem((27, 2, 8, 128), F32),
-        in_specs=[hbm, hbm, hbm, hbm, hbm, smem, hbm, hbm, hbm],
+        in_specs=[pl.BlockSpec(memory_space=pltpu.VMEM), hbm, hbm, hbm, hbm, pl.BlockSpec(memory_space=pltpu.VMEM), hbm, pl.BlockSpec(memory_space=pltpu.VMEM), pl.BlockSpec(memory_space=pltpu.VMEM)],
         out_specs=pl.BlockSpec(memory_space=pltpu.VMEM),
         scratch_shapes=[
             pltpu.SMEM((27,), F32),
@@ -541,6 +560,7 @@
             dma(()),
             dma((3,)),
             pltpu.SemaphoreType.REGULAR,
+            pltpu.SemaphoreType.REGULAR,
         ],
         compiler_params=pltpu.CompilerParams(
             collective_id=0, has_side_effects=True, vmem_limit_bytes=16 << 20

time: 28.4 us -> 28.5 us (level)
  the two profiles are of different devices: /device:TPU:8 before, /device:TPU:2 now
where the time goes in v4:
time: 28.5 us; the launch traced here: 28.2 us
  Pallas kernels  26.1 us (92%)
  local copies, waits for them, and re-layouts  1.42 us (5%)
  between operations  0.72 us (3%)
    pallas_call x1, Pallas kernels, local(): pl.pallas_call(lambda *refs: body(n_gx, n_gy, *refs), name='lattice_step'...  26.1 us
    unnamed x7, local copies, waits for them, and re-layouts  1.42 us

profile of v4, /device:TPU:2, one launch (start us, length us, event | category | flops | bytes accessed | tf_op | source)
XLA Modules:
  0.0 28.2 jit_solution(5162356722243631813)
XLA Ops:
  0.0 0.0 copy-start
  0.7 0.0 copy-start.1
  0.7 0.0 copy-start.2
  0.7 0.2 copy-done
  1.0 0.5 %copy-done.1 = s32[1,1,8,512]{3,2,1,0:T(8,128)S(1)} copy-done((s32[1,1,8,512]{3,2,1,0:T(8,128)S(1)}, s32[1,1,8,512]{3,2,1,0:T(8,128)}, u32[]{:S(2)}) %copy-start.1) | copy-done | bytes 16408
  1.4 0.0 copy-done.2
  1.5 26.1 %lattice_step.1 = f32[27,2,8,128]{3,2,1,0:T(8,128)S(1)} custom-call(f32[27,2,8,128]{3,2,1,0:T(8,128)S(1)} %copy-done, f32[27]{0:T(128)} %refs_1_.1, s32[2,8,128]{2,1,0:T(8,128)} %refs_2_.1, s32[1,1,512]{2,1,0:T(1,128)} %refs_3_.1, s32[1,1,512]{2,1,0:T(1,128)} %refs_4_.1, s32[1,512]{1,0:T(1,128)S(1)} %mark_live.1.refs_5_, s32[1,1,512]{2,1,0:T(1,128)} %refs_6_.1, ...), custom_call_target="tpu_custom_call" | custom-call | tf_op jit(solution)/shard_map/lattice_step/pallas_call | solution.py:525
  27.5 0.7 %copy.11 = f32[27,2,8,128]{3,2,1,0:T(8,128)} copy(f32[27,2,8,128]{3,2,1,0:T(8,128)S(1)} %lattice_step.1) | data formatting | bytes 442368
  (1 shorter events, 0.0 us)
Async XLA Ops:
  0.0 1.0 %copy-start = (f32[27,2,8,128]{3,2,1,0:T(8,128)S(1)}, f32[27,2,8,128]{3,2,1,0:T(8,128)}, u32[]{:S(2)}) copy-start(f32[27,2,8,128]{3,2,1,0:T(8,128)} %refs_0_.1) | copy-start | bytes 663556
  0.7 0.7 %copy-start.1 = (s32[1,1,8,512]{3,2,1,0:T(8,128)S(1)}, s32[1,1,8,512]{3,2,1,0:T(8,128)}, u32[]{:S(2)}) copy-start(s32[1,1,8,512]{3,2,1,0:T(8,128)} %refs_7_.1) | copy-start | bytes 49156
  0.7 0.8 %copy-start.2 = (f32[1,1,8,512]{3,2,1,0:T(8,128)S(1)}, f32[1,1,8,512]{3,2,1,0:T(8,128)}, u32[]{:S(2)}) copy-start(f32[1,1,8,512]{3,2,1,0:T(8,128)} %refs_8_.1) | copy-start | bytes 49156

commit v5 on v3

--- a/solution.py
+++ b/solution.py
@@ -132,6 +132,7 @@
     h_send,
     h_recv,
     ready,
+    whole,
 ):
     p = lax.axis_index("gx")
     q = lax.axis_index("gy")
@@ -160,12 +161,17 @@
     barrier = pltpu.get_barrier_semaphore()
     by_distance = sorted(range(n_gy), key=lambda k: -min(k, n_gy - k))
     targets = [(a, k) for a in (1, 0, -1) for k in by_distance if a or k]
-    greeted = [(a, k) for a in (-1, 0) for k in by_distance if a or k]
-    for a, k in greeted:
+    for k in by_distance:
         pl.semaphore_signal(
-            barrier, inc=1, device_id=(px[a + 1], around[k]), device_id_type=MESH
+            barrier, inc=1, device_id=(px[0], around[k]), device_id_type=MESH
         )
     row_id = lax.broadcasted_iota(I32, (8, 128), 0)
+
+    pl.semaphore_wait(barrier, n_gy)
+    for k in by_distance:
+        pl.semaphore_signal(
+            ready, inc=1, device_id=(px[2], around[k]), device_id_type=MESH
+        )
 
     vel = []
     for copy in loads[:3]:
@@ -258,12 +264,7 @@
     side_lines = 2 * 9 + 48 + 72 + 24
     row_lines = 2 * (24 + 16)
 
-    pl.semaphore_wait(barrier, len(greeted))
     send_samples(1)
-    for k in by_distance:
-        pl.semaphore_signal(
-            ready, inc=1, device_id=(px[2], around[k]), device_id_type=MESH
-        )
 
     for copy in loads[4:]:
         copy.wait()
@@ -317,11 +318,19 @@
                 rows[base + 27 + 9 * (1 - x) + k] = value
 
     send_side(0)
+    def greet():
+        pl.semaphore_wait(ready, n_gy)
+        pl.semaphore_signal(whole, inc=1, device_id=(px[0], q), device_id_type=MESH)
+
+    def send_back():
+        send_samples(-1)
+        send_side(1)
+
+    pl.when(p != 0)(greet)
+    pl.semaphore_wait(whole, 1)
     send_samples(0)
     send_row()
-    pl.semaphore_wait(ready, n_gy)
-    send_samples(-1)
-    send_side(1)
+    pl.when(p != 0)(send_back)
 
     chunk = [0, 1 - par, 1]
     half = [1 - par, par, 1 - par]
@@ -479,6 +488,11 @@
     side(1)
     edge_rows(found, parts, table_near, 0)
     finish(False)
+
+    @pl.when(p == 0)
+    def _():
+        greet()
+        send_back()
 
     arrived(h_recv.at[0], side_lines)
     block_plane(0, solid_x[0])
@@ -541,6 +555,7 @@
             dma(()),
             dma((3,)),
             pltpu.SemaphoreType.REGULAR,
+            pltpu.SemaphoreType.REGULAR,
         ],
         compiler_params=pltpu.CompilerParams(
             collective_id=0, has_side_effects=True, vmem_limit_bytes=16 << 20

time: 28.4 us -> 27.9 us (0.982)
  the two profiles are of different devices: /device:TPU:8 before, /device:TPU:2 now
where the time goes in v5:
time: 27.9 us; the launch traced here: 27.8 us
  Pallas kernels  26.4 us (95%)
  local copies, waits for them, and re-layouts  0.69 us (2%)
  between operations  0.66 us (2%)
    pallas_call x1, Pallas kernels, local(): pl.pallas_call(lambda *refs: body(n_gx, n_gy, *refs), name='lattice_step'...  26.4 us
    unnamed x1, local copies, waits for them, and re-layouts  0.69 us

profile of v5, /device:TPU:2, one launch (start us, length us, event | category | flops | bytes accessed | tf_op | source)
XLA Modules:
  0.0 27.8 jit_solution(9836013297027734206)
XLA Ops:
  0.7 26.4 %lattice_step.1 = f32[27,2,8,128]{3,2,1,0:T(8,128)S(1)} custom-call(f32[27,2,8,128]{3,2,1,0:T(8,128)} %refs_0_.1, f32[27]{0:T(128)} %refs_1_.1, s32[2,8,128]{2,1,0:T(8,128)} %refs_2_.1, s32[1,1,512]{2,1,0:T(1,128)} %refs_3_.1, s32[1,1,512]{2,1,0:T(1,128)} %refs_4_.1, s32[1,1]{1,0:T(1,128)S(6)} %copy.12.refs_5_, s32[1,1,512]{2,1,0:T(1,128)} %refs_6_.1, ...), custom_call_target="tpu_custom_call" | custom-call | tf_op jit(solution)/shard_map/lattice_step/pallas_call | solution.py:520
  27.1 0.7 %copy.11 = f32[27,2,8,128]{3,2,1,0:T(8,128)} copy(f32[27,2,8,128]{3,2,1,0:T(8,128)S(1)} %lattice_step.1) | data formatting | bytes 442368

commit v6 on v5

--- a/solution.py
+++ b/solution.py
@@ -187,8 +187,6 @@
         fields[0, x] = rho
         for k in range(3):
             fields[k + 1, x] = u[k]
-        for m in range(27):
-            part[m, x] = f[m]
 
     for j in range(4):
         total = [jnp.zeros((8, 128), F32) for _ in range(3)]
@@ -293,7 +291,9 @@
 
     loads[3].wait()
     for x in range(2):
-        f = [part[m, x] for m in range(27)]
+        f = [pop[i, x] * weight[i] for i in range(27)]
+        for axis in (2, 1, 0):
+            f = along(f, axis, to_moments)
         balance = equilibrium_moments(fields[0, x], [fields[1 + k, x] for k in range(3)])
         for m in range(27):
             off = f[m] if balance[m] is None else f[m] - balance[m]

time: 27.9 us -> 27.9 us (level)
  no operation moved by 1% of the time
where the time goes in v6:
time: 27.9 us; the launch traced here: 27.7 us
  Pallas kernels  26.4 us (95%)
  local copies, waits for them, and re-layouts  0.69 us (2%)
  between operations  0.66 us (2%)
    pallas_call x1, Pallas kernels, local(): pl.pallas_call(lambda *refs: body(n_gx, n_gy, *refs), name='lattice_step'...  26.4 us
    unnamed x1, local copies, waits for them, and re-layouts  0.69 us

profile of v6, /device:TPU:2, one launch (start us, length us, event | category | flops | bytes accessed | tf_op | source)
XLA Modules:
  0.0 27.7 jit_solution(12355181547083344059)
XLA Ops:
  0.7 26.4 %lattice_step.1 = f32[27,2,8,128]{3,2,1,0:T(8,128)S(1)} custom-call(f32[27,2,8,128]{3,2,1,0:T(8,128)} %refs_0_.1, f32[27]{0:T(128)} %refs_1_.1, s32[2,8,128]{2,1,0:T(8,128)} %refs_2_.1, s32[1,1,512]{2,1,0:T(1,128)} %refs_3_.1, s32[1,1,512]{2,1,0:T(1,128)} %refs_4_.1, s32[1,1]{1,0:T(1,128)S(6)} %copy.12.refs_5_, s32[1,1,512]{2,1,0:T(1,128)} %refs_6_.1, ...), custom_call_target="tpu_custom_call" | custom-call | tf_op jit(solution)/shard_map/lattice_step/pallas_call | solution.py:520
  27.1 0.7 %copy.11 = f32[27,2,8,128]{3,2,1,0:T(8,128)} copy(f32[27,2,8,128]{3,2,1,0:T(8,128)S(1)} %lattice_step.1) | data formatting | bytes 442368

commit v7 on v6

--- a/solution.py
+++ b/solution.py
@@ -262,7 +262,8 @@
     side_lines = 2 * 9 + 48 + 72 + 24
     row_lines = 2 * (24 + 16)
 
-    send_samples(1)
+    odd = lax.rem(p, 2)
+    pl.when(odd == 1)(lambda: send_samples(1))
 
     for copy in loads[4:]:
         copy.wait()
@@ -318,6 +319,7 @@
                 rows[base + 27 + 9 * (1 - x) + k] = value
 
     send_side(0)
+    pl.when(odd == 0)(lambda: send_samples(1))
     def greet():
         pl.semaphore_wait(ready, n_gy)
         pl.semaphore_signal(whole, inc=1, device_id=(px[0], q), device_id_type=MESH)

time: 27.9 us -> 27.9 us (level)
  no operation moved by 1% of the time
where the time goes in v7:
time: 27.9 us; the launch traced here: 27.7 us
  Pallas kernels  26.4 us (95%)
  local copies, waits for them, and re-layouts  0.69 us (2%)
  between operations  0.66 us (2%)
    pallas_call x1, Pallas kernels, local(): pl.pallas_call(lambda *refs: body(n_gx, n_gy, *refs), name='lattice_step'...  26.4 us
    unnamed x1, local copies, waits for them, and re-layouts  0.69 us

profile of v7, /device:TPU:2, one launch (start us, length us, event | category | flops | bytes accessed | tf_op | source)
XLA Modules:
  0.0 27.7 jit_solution(10020696842000570812)
XLA Ops:
  0.7 26.4 %lattice_step.1 = f32[27,2,8,128]{3,2,1,0:T(8,128)S(1)} custom-call(f32[27,2,8,128]{3,2,1,0:T(8,128)} %refs_0_.1, f32[27]{0:T(128)} %refs_1_.1, s32[2,8,128]{2,1,0:T(8,128)} %refs_2_.1, s32[1,1,512]{2,1,0:T(1,128)} %refs_3_.1, s32[1,1,512]{2,1,0:T(1,128)} %refs_4_.1, s32[1,1]{1,0:T(1,128)S(6)} %copy.12.refs_5_, s32[1,1,512]{2,1,0:T(1,128)} %refs_6_.1, ...), custom_call_target="tpu_custom_call" | custom-call | tf_op jit(solution)/shard_map/lattice_step/pallas_call | solution.py:522
  27.1 0.7 %copy.11 = f32[27,2,8,128]{3,2,1,0:T(8,128)} copy(f32[27,2,8,128]{3,2,1,0:T(8,128)S(1)} %lattice_step.1) | data formatting | bytes 442368
